TPU v7x, 8 devices: a whole 2x2x1 slice. The times are simulated.
8 devices in a mesh: replica: 4 (over z, y, x), data: 2 (over core).
Axes of the slice: x: 2, y: 2, z: 1, core: 2. Of those that a mesh axis runs over, the one named last changes fastest.
Arguments:
- x_seq: bfloat16 [256, 16, 1024], P(('replica', 'data'))
- dy_seq: float32 [256, 16, 1024], P(('replica', 'data'))
- w_stack: bfloat16 [6, 2048, 4096], replicated
- b_stack: float32 [6, 4096], replicated
Outputs:
- output 1: float32 [6, 2048, 4096], replicated
- output 2: float32 [6, 4096], replicated
- output 3: float32 [256, 16, 1024], P(('replica', 'data'))
All inputs are finite; a program needn't handle non-finite values.
Results may differ from a plain program's by a relative error of at most 0.0156497.
Values are sent between devices in bfloat16 or wider.
A program may use at most 1.25 GiB of HBM per device.

v0:
```python
import jax
import jax.numpy as jnp
from jax import lax
from jax.sharding import PartitionSpec as P


def layer_forward(u_seq, w_layer, b_layer):
    hidden = u_seq.shape[-1]
    batch_rows = u_seq.shape[1]
    w_rec = w_layer[hidden:]
    in_proj = jnp.einsum('tbh,hg->tbg', u_seq, w_layer[:hidden], preferred_element_type=jnp.float32) + b_layer

    def time_step(carry_state, z_in):
        h_prev, c_prev = carry_state
        z_all = z_in + jnp.dot(h_prev, w_rec, preferred_element_type=jnp.float32)
        z_i, z_f, z_g, z_o = jnp.split(z_all, 4, axis=-1)
        gate_i = jax.nn.sigmoid(z_i)
        gate_f = jax.nn.sigmoid(z_f)
        gate_g = jnp.tanh(z_g)
        gate_o = jax.nn.sigmoid(z_o)
        c_new = gate_f * c_prev + gate_i * gate_g
        tanh_c = jnp.tanh(c_new)
        h_new = (gate_o * tanh_c).astype(jnp.bfloat16)
        return (h_new, c_new), (h_new, c_new, tanh_c, gate_i, gate_f, gate_g, gate_o)

    init_state = (jnp.zeros((batch_rows, hidden), jnp.bfloat16), jnp.zeros((batch_rows, hidden), jnp.float32))
    return lax.scan(time_step, init_state, in_proj)[1]


def layer_backward(u_seq, w_layer, saved_acts, dh_seq):
    hidden = u_seq.shape[-1]
    h_seq, c_seq, tanh_seq, i_seq, f_seq, g_seq, o_seq = saved_acts
    h_prev_seq = jnp.concatenate([jnp.zeros_like(h_seq[:1]), h_seq[:-1]], axis=0)
    c_prev_seq = jnp.concatenate([jnp.zeros_like(c_seq[:1]), c_seq[:-1]], axis=0)
    w_rec = w_layer[hidden:]

    def time_step(carry_state, step_in):
        dh_rec, dc_next = carry_state
        dh_out, c_prev, tanh_c, gate_i, gate_f, gate_g, gate_o = step_in
        dh_tot = dh_out + dh_rec
        dc_cur = dc_next + dh_tot * gate_o * (1.0 - tanh_c * tanh_c)
        dz_all = jnp.concatenate([dc_cur * gate_g * gate_i * (1.0 - gate_i), dc_cur * c_prev * gate_f * (1.0 - gate_f), dc_cur * gate_i * (1.0 - gate_g * gate_g), dh_tot * tanh_c * gate_o * (1.0 - gate_o)], axis=-1)
        dz_low = dz_all.astype(jnp.bfloat16)
        dh_prev = jnp.einsum('bg,hg->bh', dz_low, w_rec, preferred_element_type=jnp.float32)
        return (dh_prev, dc_cur * gate_f), (dz_low, jnp.sum(dz_all, axis=0))

    init_state = (jnp.zeros_like(dh_seq[0]), jnp.zeros_like(dh_seq[0]))
    dz_seq, db_steps = lax.scan(time_step, init_state, (dh_seq, c_prev_seq, tanh_seq, i_seq, f_seq, g_seq, o_seq), reverse=True)[1]
    dx_seq = jnp.einsum('tbg,hg->tbh', dz_seq, w_layer[:hidden], preferred_element_type=jnp.float32)
    dw_in = jnp.einsum('tbh,tbg->hg', u_seq, dz_seq, preferred_element_type=jnp.float32)
    dw_rec = jnp.einsum('tbh,tbg->hg', h_prev_seq, dz_seq, preferred_element_type=jnp.float32)
    return jnp.concatenate([dw_in, dw_rec], axis=0), jnp.sum(db_steps, axis=0), dx_seq


def reduce_weights(dw_part):
    part_low = dw_part.astype(jnp.bfloat16)
    shard_sum = lax.psum_scatter(part_low, 'data', scatter_dimension=0, tiled=True)
    shard_sum = lax.psum(shard_sum, 'replica')
    return lax.all_gather(shard_sum, 'data', axis=0, tiled=True).astype(jnp.float32)


def solution(mesh):
    batch_axes = ('replica', 'data')

    def local_grads(x_loc, dy_loc, w_stack, b_stack):
        layers = w_stack.shape[0]
        u_seq = jnp.swapaxes(x_loc, 0, 1)
        layer_inputs = []
        layer_saved = []
        for layer_idx in range(layers):
            saved_acts = layer_forward(u_seq, w_stack[layer_idx], b_stack[layer_idx])
            layer_inputs.append(u_seq)
            layer_saved.append(saved_acts)
            u_seq = saved_acts[0]
        dh_seq = jnp.swapaxes(dy_loc, 0, 1)
        dw_list = []
        db_list = []
        for layer_idx in reversed(range(layers)):
            dw_part, db_part, dh_seq = layer_backward(layer_inputs[layer_idx], w_stack[layer_idx], layer_saved[layer_idx], dh_seq)
            dw_list.append(reduce_weights(dw_part))
            db_list.append(lax.psum(db_part.astype(jnp.bfloat16), batch_axes).astype(jnp.float32))
        return jnp.stack(dw_list[::-1]), jnp.stack(db_list[::-1]), jnp.swapaxes(dh_seq, 0, 1)

    return jax.shard_map(local_grads, mesh=mesh, in_specs=(P(batch_axes), P(batch_axes), P(), P()), out_specs=(P(), P(), P(batch_axes)), check_vma=False)
```

profile of v0, /device:TPU:0, one launch (start us, length us, event | category | flops | bytes accessed | tf_op | source)
XLA Modules:
  0.0 3048.0 jit_solution(18302625240941671879)
XLA Ops:
  13.5 33.4 %slice_bitcast_fusion = (bf16[1024,4096]{1,0:T(8,128)(2,1)}, bf16[1024,4096]{1,0:T(8,128)(2,1)}, bf16[1024,4096]{1,0:T(8,128)(2,1)}, bf16[1024,4096]{1,0:T(8,128...) fusion(bf16[6,2048,4096]{2,1,0:T(8,128)(2,1)} %param.30), kind=kLoop, calls=%fused_computation.414 | loop fusion | bytes 100663296 | tf_op jit(solution)/shard_map/slice | solution.py:10
  66.4 105.7 %while.288 = (s32[]{:T(128)}, bf16[32,1024]{1,0:T(8,128)(2,1)S(1)}, f32[32,1024]{1,0:T(8,128)S(1)}, bf16[16,32,1024]{2,1,0:T(8,128)(2,1)}, f32[16,32,1024]{2,1,0...) while((s32[]{:T(128)}, bf16[32,1024]{1,0:T(8,128)(2,1)S(1)}, ...), condition=%wide.region_1.2_spmd.clone, body=%wide.region_0.1_spmd.clone.sunk | while | flops 269189120 | bytes 11600040 | solution.py:27
  194.0 106.0 %while.289 = (s32[]{:T(128)}, bf16[32,1024]{1,0:T(8,128)(2,1)S(1)}, f32[32,1024]{1,0:T(8,128)S(1)}, bf16[16,32,1024]{2,1,0:T(8,128)(2,1)}, f32[16,32,1024]{2,1,0...) while((s32[]{:T(128)}, bf16[32,1024]{1,0:T(8,128)(2,1)S(1)}, ...), condition=%wide.region_3.4_spmd.clone, body=%wide.region_2.3_spmd.clone.sunk | while | flops 269189120 | bytes 11600040 | solution.py:27
  321.7 106.5 %while.290 = (s32[]{:T(128)}, bf16[32,1024]{1,0:T(8,128)(2,1)S(1)}, f32[32,1024]{1,0:T(8,128)S(1)}, bf16[16,32,1024]{2,1,0:T(8,128)(2,1)}, f32[16,32,1024]{2,1,0...) while((s32[]{:T(128)}, bf16[32,1024]{1,0:T(8,128)(2,1)S(1)}, ...), condition=%wide.region_5.6_spmd.clone, body=%wide.region_4.5_spmd.clone.sunk | while | flops 269189120 | bytes 11600040 | solution.py:27
  449.0 95.8 %while.291 = (s32[]{:T(128)}, bf16[32,1024]{1,0:T(8,128)(2,1)S(1)}, f32[32,1024]{1,0:T(8,128)S(1)}, bf16[16,32,1024]{2,1,0:T(8,128)(2,1)S(1)}, f32[16,32,1024]{2...) while((s32[]{:T(128)}, bf16[32,1024]{1,0:T(8,128)(2,1)S(1)}, ...), condition=%wide.region_7.8_spmd.clone, body=%wide.region_6.7_spmd.clone.sunk | while | flops 269189120 | bytes 11600040 | solution.py:27
  564.4 96.8 %while.292 = (s32[]{:T(128)}, bf16[32,1024]{1,0:T(8,128)(2,1)S(1)}, f32[32,1024]{1,0:T(8,128)S(1)}, bf16[16,32,1024]{2,1,0:T(8,128)(2,1)S(1)}, f32[16,32,1024]{2...) while((s32[]{:T(128)}, bf16[32,1024]{1,0:T(8,128)(2,1)S(1)}, ...), condition=%wide.region_9.10_spmd.clone, body=%wide.region_8.9_spmd.clone.sunk | while | flops 269189120 | bytes 11600040 | solution.py:27
  681.0 96.0 %while.293 = (s32[]{:T(128)}, bf16[32,1024]{1,0:T(8,128)(2,1)S(1)}, f32[32,1024]{1,0:T(8,128)S(1)}, bf16[16,32,1024]{2,1,0:T(8,128)(2,1)S(1)}, f32[16,32,1024]{2...) while((s32[]{:T(128)}, bf16[32,1024]{1,0:T(8,128)(2,1)S(1)}, ...), condition=%wide.region_11.12_spmd.clone, body=%wide.region_10.11_spmd.clone.sunk | while | flops 269189120 | bytes 11600040 | solution.py:27
  781.0 152.1 %while.294 = (s32[]{:T(128)}, f32[32,1024]{1,0:T(8,128)S(1)}, f32[32,1024]{1,0:T(8,128)S(1)}, bf16[16,32,4096]{2,1,0:T(8,128)(2,1)}, f32[16,4096]{1,0:T(8,128)S(...) while((s32[]{:T(128)}, f32[32,1024]{1,0:T(8,128)S(1)}, ...), condition=%wide.region_14.15_spmd.clone, body=%wide.region_12.14_spmd.clone.sunk | while | flops 271970304 | bytes 12763331 | solution.py:48
  966.2 151.9 %while.295 = (s32[]{:T(128)}, f32[32,1024]{1,0:T(8,128)S(1)}, f32[32,1024]{1,0:T(8,128)S(1)}, bf16[16,32,4096]{2,1,0:T(8,128)(2,1)}, f32[16,4096]{1,0:T(8,128)S(...) while((s32[]{:T(128)}, f32[32,1024]{1,0:T(8,128)S(1)}, ...), condition=%wide.region_17.18_spmd.clone, body=%wide.region_15.17_spmd.clone.sunk | while | flops 271970304 | bytes 12763331 | solution.py:48
  1151.3 151.9 %while.296 = (s32[]{:T(128)}, f32[32,1024]{1,0:T(8,128)S(1)}, f32[32,1024]{1,0:T(8,128)S(1)}, bf16[16,32,4096]{2,1,0:T(8,128)(2,1)}, f32[16,4096]{1,0:T(8,128)S(...) while((s32[]{:T(128)}, f32[32,1024]{1,0:T(8,128)S(1)}, ...), condition=%wide.region_20.21_spmd.clone, body=%wide.region_18.20_spmd.clone.sunk | while | flops 271970304 | bytes 12763331 | solution.py:48
  1336.6 151.7 %while.297 = (s32[]{:T(128)}, f32[32,1024]{1,0:T(8,128)S(1)}, f32[32,1024]{1,0:T(8,128)S(1)}, bf16[16,32,4096]{2,1,0:T(8,128)(2,1)}, f32[16,4096]{1,0:T(8,128)S(...) while((s32[]{:T(128)}, f32[32,1024]{1,0:T(8,128)S(1)}, ...), condition=%wide.region_23.24_spmd.clone, body=%wide.region_21.23_spmd.clone.sunk | while | flops 271970304 | bytes 12763331 | solution.py:48
  1521.6 151.7 %while.298 = (s32[]{:T(128)}, f32[32,1024]{1,0:T(8,128)S(1)}, f32[32,1024]{1,0:T(8,128)S(1)}, bf16[16,32,4096]{2,1,0:T(8,128)(2,1)}, f32[16,4096]{1,0:T(8,128)S(...) while((s32[]{:T(128)}, f32[32,1024]{1,0:T(8,128)S(1)}, ...), condition=%wide.region_26.27_spmd.clone, body=%wide.region_24.26_spmd.clone.sunk | while | flops 271970304 | bytes 12763331 | solution.py:48
  1706.4 151.8 %while.299 = (s32[]{:T(128)}, f32[32,1024]{1,0:T(8,128)S(1)}, f32[32,1024]{1,0:T(8,128)S(1)}, bf16[16,32,4096]{2,1,0:T(8,128)(2,1)}, f32[16,4096]{1,0:T(8,128)S(...) while((s32[]{:T(128)}, f32[32,1024]{1,0:T(8,128)S(1)}, ...), condition=%wide.region_29.30_spmd.clone, body=%wide.region_27.29_spmd.clone.sunk | while | flops 271970304 | bytes 12763331 | solution.py:48
  1877.7 24.6 reduce-scatter.7.cloned.1.call-done
  1902.4 845.3 %all-reduce.16.cloned.1.call-done = (bf16[1024,4096]{1,0:T(8,128)(2,1)}, bf16[1024,4096]{1,0:T(8,128)(2,1)}, bf16[1024,4096]{1,0:T(8,128)(2,1)}, bf16[1024,4096]...) async-done(((bf16[1024,4096]{1,0:T(8,128)(2,1)}, bf16[1024,4096]{1,0:T(8,128)(2,1)}, bf16[1024,4096]{1,0:T(8,128)(2,1)}, ...) | async-done | bytes 50331664 | tf_op jit(solution)/shard_map/psum | solution.py:58
  2752.0 26.0 all-reduce.12
  2823.9 16.4 all-gather.11.cloned.1.call-done
  2840.3 14.0 bitcast_dynamic-update-slice_fusion.45
  2854.3 16.5 all-gather.13.cloned.1.call-done
  2870.9 14.0 bitcast_dynamic-update-slice_fusion.44
  2884.9 16.4 all-gather.15.cloned.1.call-done
  2915.2 16.5 all-gather.17.cloned.1.call-done
  2931.8 14.0 bitcast_dynamic-update-slice_fusion.42
  2945.8 95.3 %stack.67 = f32[6,2048,4096]{2,1,0:T(8,128)} convert(bf16[6,2048,4096]{2,1,0:T(8,128)(2,1)} %bitcast_dynamic-update-slice_fusion.42) | non-fusion elementwise | flops 50331648 | bytes 301989888 | tf_op jit(solution)/shard_map/stack | solution.py:82
  (1225 shorter events, 1894.2 us)
Async XLA Ops:
  7.2 1870.4 %reduce-scatter.17.cloned.1.call-start = ((), (), s32[]{:S(2)}) async-start(), calls=%async_computation.16 | async-start | bytes 25165824 | tf_op jit(solution)/shard_map/reduce_scatter | solution.py:57
  13.5 33.4 %copy-start.45 = (bf16[32,16,1024]{2,1,0:T(8,128)(2,1)S(1)}, bf16[32,16,1024]{2,1,0:T(8,128)(2,1)}, u32[]{:S(2)}) copy-start(bf16[32,16,1024]{2,1,0:T(8,128)(2,1)} %param.28) | copy-start | bytes 3145732
  172.1 12.4 copy-start.3
  300.0 12.4 copy-start.5
  428.2 12.4 copy-start.7
  449.0 95.9 %copy-start.44 = (f32[1,4096]{1,0:T(1,128)S(1)}, f32[1,4096]{1,0:T(1,128)}, u32[]{:S(2)}) copy-start(f32[1,4096]{1,0:T(1,128)} %get-tuple-element.2957) | copy-start | bytes 49156
  544.9 11.2 copy-start.9
  544.9 11.2 copy-start.28
  564.4 96.9 %copy-start.43 = (f32[1,4096]{1,0:T(1,128)S(1)}, f32[1,4096]{1,0:T(1,128)}, u32[]{:S(2)}) copy-start(f32[1,4096]{1,0:T(1,128)} %get-tuple-element.2952) | copy-start | bytes 49156
  661.3 11.3 copy-start.11
  661.3 11.2 copy-start.30
  952.5 925.1 %reduce-scatter.15.cloned.1.call-start = ((), (), s32[]{:S(2)}) async-start(), calls=%async_computation.14 | async-start | bytes 25165824 | tf_op jit(solution)/shard_map/reduce_scatter | solution.py:57
  1137.6 740.0 %reduce-scatter.13.cloned.1.call-start = ((), (), s32[]{:S(2)}) async-start(), calls=%async_computation.12 | async-start | bytes 25165824 | tf_op jit(solution)/shard_map/reduce_scatter | solution.py:57
  1137.7 10.6 copy-start.10
  1322.5 555.1 %reduce-scatter.11.cloned.1.call-start = ((), (), s32[]{:S(2)}) async-start(), calls=%async_computation.10 | async-start | bytes 25165824 | tf_op jit(solution)/shard_map/reduce_scatter | solution.py:57
  1507.7 370.0 %reduce-scatter.9.cloned.1.call-start = ((), (), s32[]{:S(2)}) async-start(), calls=%async_computation.8 | async-start | bytes 25165824 | tf_op jit(solution)/shard_map/reduce_scatter | solution.py:57
  1692.6 209.7 %reduce-scatter.7.cloned.1.call-start = ((), (), s32[]{:S(2)}) async-start(), calls=%async_computation.6 | async-start | bytes 25165824 | tf_op jit(solution)/shard_map/reduce_scatter | solution.py:57
  1877.5 870.2 %all-reduce.16.cloned.1.call-start = ((), (), s32[]{:S(2)}) async-start(), calls=%async_computation.18 | async-start | bytes 100663296 | tf_op jit(solution)/shard_map/psum | solution.py:58
  1902.4 887.3 %all-gather.7.cloned.1.call-start = ((), (), s32[]{:S(2)}) async-start(), calls=%async_computation.7 | async-start | bytes 25165824 | tf_op jit(solution)/shard_map/all_gather | solution.py:59
  2747.7 62.2 %all-gather.9.cloned.1.call-start = ((), (), s32[]{:S(2)}) async-start(), calls=%async_computation.9 | async-start | bytes 25165824 | tf_op jit(solution)/shard_map/all_gather | solution.py:59
  2748.4 91.9 %all-gather.11.cloned.1.call-start = ((), (), s32[]{:S(2)}) async-start(), calls=%async_computation.11 | async-start | bytes 25165824 | tf_op jit(solution)/shard_map/all_gather | solution.py:59
  2749.0 121.8 %all-gather.13.cloned.1.call-start = ((), (), s32[]{:S(2)}) async-start(), calls=%async_computation.13 | async-start | bytes 25165824 | tf_op jit(solution)/shard_map/all_gather | solution.py:59
  2749.8 151.5 %all-gather.15.cloned.1.call-start = ((), (), s32[]{:S(2)}) async-start(), calls=%async_computation.15 | async-start | bytes 25165824 | tf_op jit(solution)/shard_map/all_gather | solution.py:59
  2750.3 181.4 %all-gather.17.cloned.1.call-start = ((), (), s32[]{:S(2)}) async-start(), calls=%async_computation.17 | async-start | bytes 25165824 | tf_op jit(solution)/shard_map/all_gather | solution.py:59
  (35 other events, 199.2 us)
Sparse Core Ops, SparseCore 0:
  952.7 24.6 reduce-scatter.16
  1137.7 24.6 reduce-scatter.14
  1322.7 24.6 reduce-scatter.12
  1507.8 24.6 reduce-scatter.10
  1692.7 24.6 reduce-scatter.8
  1877.6 24.6 reduce-scatter.6
  1906.9 840.7 all-reduce.15
  2749.2 30.1 all-gather.6
  2780.9 28.9 all-gather.8
  2811.3 28.9 all-gather.10
  2841.8 28.9 all-gather.12
  2872.2 28.9 all-gather.14
  2902.7 28.9 all-gather.16
where the time goes:
time: 3070 us; the launch traced here: 3050 us
  matrix products  1250 us (41%)
  waiting for transfers between devices  945 us (31%)
  other arithmetic  562 us (18%)
  local copies, waits for them, and re-layouts  240 us (8%)
    psum x1, waiting for transfers between devices, reduce_weights(): shard_sum = lax.psum(shard_sum, 'replica')  845 us
    dot_general x96, matrix products, time_step(): jnp.einsum('bg,hg->bh', dz_low, w_rec, preferred_element_type=jnp.float32)  572 us
    dot_general x96, matrix products, time_step(): z_all = z_in + jnp.dot(h_prev, w_rec, preferred_element_type=jnp.float32)  479 us
    concatenate x192, other arithmetic, time_step(): jnp.concatenate([dc_cur * gate_g * gate_i * (1.0 - gate_i), dc_cur * c_pr...  224 us
    dynamic_update_slice x192, other arithmetic, layer_forward(): return lax.scan(time_step, init_state, in_proj)[1]  123 us
    another operation x1, other arithmetic, local_grads(): jnp.stack(dw_list[::-1])  95.3 us
    unnamed x99, local copies, waits for them, and re-layouts  80.6 us
    all_gather x6, waiting for transfers between devices, reduce_weights(): lax.all_gather(shard_sum, 'data', axis=0, tiled=True).astype(jnp.float32)  72.1 us
  transfers between devices with their start and end apart: 13, of which 7 were waited for; matrix products, arithmetic and copies ran while one was open for 33% of the time, Pallas kernels for 0%

commit v1 on v0

v1 whole, which is shorter than its diff:
```python
import functools

import jax
import jax.numpy as jnp
from jax import lax
from jax.experimental import pallas as pl
from jax.experimental.pallas import tpu as pltpu
from jax.sharding import PartitionSpec as P

VMEM_LIMIT = 62 * 1024 * 1024
CHIPS = 4
PEERS = 8
EXTRA = 16
NT = (((1,), (1,)), ((), ()))
MESH = pl.DeviceIdType.MESH


def sigmoid(z):
    return 0.5 * jnp.tanh(0.5 * z) + 0.5


def forward_kernel(layer, steps, rows, hidden, u_ref, w_hbm, b_ref, gates_hbm, c_hbm, h_ref, w_in, w_rec, gates, c_buf, w_sem, out_sem):
    tile = 512
    tiles = 4 * hidden // tile

    def in_copy(j):
        cols = pl.ds(j * tile, tile)
        return pltpu.make_async_copy(w_hbm.at[layer, pl.ds(0, hidden), cols], w_in.at[:, cols], w_sem.at[j])

    for j in range(tiles):
        in_copy(j).start()
    rec_copy = pltpu.make_async_copy(w_hbm.at[layer, pl.ds(hidden, hidden)], w_rec, w_sem.at[tiles])
    rec_copy.start()
    for j in range(tiles):
        cols = pl.ds(j * tile, tile)
        in_copy(j).wait()
        gates[:, cols] = jnp.dot(u_ref[...], w_in[:, cols], preferred_element_type=jnp.float32) + b_ref[0, :, cols]
    rec_copy.wait()
    part = 256

    def out_copies(t):
        r = pl.ds(pl.multiple_of(t * rows, rows), rows)
        return (pltpu.make_async_copy(gates.at[r], gates_hbm.at[r], out_sem.at[0]), pltpu.make_async_copy(c_buf.at[r], c_hbm.at[r], out_sem.at[1]))

    def step(t, first):
        r = pl.ds(pl.multiple_of(t * rows, rows), rows)
        if not first:
            rp = pl.ds(pl.multiple_of((t - 1) * rows, rows), rows)
            h_prev = h_ref[rp, :]
            for copy in out_copies(t - 1):
                copy.start()
        for p in range(hidden // part):
            z = []
            for k in range(4):
                cols = pl.ds(k * hidden + p * part, part)
                zk = gates[r, cols]
                if not first:
                    zk = zk + jnp.dot(h_prev, w_rec[:, cols], preferred_element_type=jnp.float32)
                z.append(zk)
            pc = pl.ds(p * part, part)
            gate_i, gate_f, gate_g, gate_o = sigmoid(z[0]), sigmoid(z[1]), jnp.tanh(z[2]), sigmoid(z[3])
            c_new = gate_i * gate_g
            if not first:
                c_new = gate_f * c_buf[rp, pc] + c_new
            for k, v in enumerate((gate_i, gate_f, gate_g, gate_o)):
                gates[r, pl.ds(k * hidden + p * part, part)] = v
            c_buf[r, pc] = c_new
            h_ref[r, pc] = (gate_o * jnp.tanh(c_new)).astype(jnp.bfloat16)

    step(0, True)

    @pl.loop(1, steps)
    def _(t):
        step(t, False)

    for copy in out_copies(steps - 1):
        copy.start()
    pltpu.make_async_copy(gates, gates_hbm, out_sem.at[0]).wait()
    pltpu.make_async_copy(c_buf, c_hbm, out_sem.at[1]).wait()


def forward(layer, u, w_stack, b_stack, steps):
    n, hidden = u.shape
    width = 4 * hidden
    whole = pl.BlockSpec(memory_space=pltpu.VMEM)
    anywhere = pl.BlockSpec(memory_space=pl.ANY)
    return pl.pallas_call(
        functools.partial(forward_kernel, layer, steps, n // steps, hidden),
        grid=(1,),
        in_specs=[
            pl.BlockSpec((n, hidden), lambda i: (0, 0)),
            anywhere,
            pl.BlockSpec((1, 1, width), lambda i: (layer, 0, 0)),
        ],
        out_specs=[anywhere, anywhere, pl.BlockSpec((n, hidden), lambda i: (0, 0))],
        out_shape=[
            jax.ShapeDtypeStruct((n, width), jnp.float32),
            jax.ShapeDtypeStruct((n, hidden), jnp.float32),
            jax.ShapeDtypeStruct((n, hidden), jnp.bfloat16),
        ],
        scratch_shapes=[
            pltpu.VMEM((hidden, width), jnp.bfloat16),
            pltpu.VMEM((hidden, width), jnp.bfloat16),
            pltpu.VMEM((n, width), jnp.float32),
            pltpu.VMEM((n, hidden), jnp.float32),
            pltpu.SemaphoreType.DMA((9,)),
            pltpu.SemaphoreType.DMA((2,)),
        ],
        compiler_params=pltpu.CompilerParams(vmem_limit_bytes=VMEM_LIMIT),
        cost_estimate=pl.CostEstimate(flops=2 * n * 2 * hidden * width * 4, bytes_accessed=2 * 2 * hidden * width, transcendentals=0),
        name="lstm_forward",
    )(u, w_stack, b_stack)


def backward_kernel(layer, steps, rows, hidden, e_ref, gates_ref, c_ref, cp_ref, w_hbm, land, dx_ref, r_buf, dc_buf, db_buf, dz_buf, w_in, w_rec, w_sem, own_sem, send_sem, recv_sem):
    s = pl.program_id(0)
    t = steps - 1 - s
    width = 4 * hidden
    share = width // PEERS
    n = steps * rows
    chip = lax.axis_index("replica")
    core = lax.axis_index("data")
    chips = (chip, chip + 1 - 2 * lax.rem(chip, 2), lax.rem(chip + 2, 4), 3 - chip)
    cores = (core, 1 - core)
    rec_copy = pltpu.make_async_copy(w_hbm.at[layer, pl.ds(hidden, hidden)], w_rec, w_sem.at[0])
    in_copy = pltpu.make_async_copy(w_hbm.at[layer, pl.ds(0, hidden)], w_in, w_sem.at[1])

    def own_copy(start, count):
        r = pl.ds(start, count)
        cols = pl.ds(pl.multiple_of((chip * 2 + core) * share, share), share)
        return pltpu.make_async_copy(dz_buf.at[r, cols], land.at[chip, r], own_sem)

    def send_copy(k, start, count):
        to_chip, to_core = chips[k % 4], cores[k // 4]
        r = pl.ds(start, count)
        cols = pl.ds(pl.multiple_of((to_chip * 2 + to_core) * share, share), share)
        return pltpu.make_async_remote_copy(
            src_ref=dz_buf.at[r, cols],
            dst_ref=land.at[chip + 4 * (k // 4), r],
            send_sem=send_sem.at[k],
            recv_sem=recv_sem.at[k],
            device_id=(to_chip, to_core),
            device_id_type=MESH,
        )

    def send(start, count):
        for k in (3, 7, 1, 2, 5, 6, 4):
            send_copy(k, start, count).start()
        own_copy(start, count).start()

    @pl.when(s == 0)
    def _():
        rec_copy.start()
        in_copy.start()
        barrier = pltpu.get_barrier_semaphore()
        for k in range(1, PEERS):
            pl.semaphore_signal(barrier, inc=1, device_id=(chips[k % 4], cores[k // 4]), device_id_type=MESH)
        r_buf[...] = jnp.zeros_like(r_buf)
        dc_buf[...] = jnp.zeros_like(dc_buf)
        db_buf[...] = jnp.zeros_like(db_buf)
        rec_copy.wait()
        pl.semaphore_wait(barrier, PEERS - 1)

    for q in range(1, 4):
        @pl.when(s == 4 * q)
        def _():
            send(n - 4 * q * rows, 4 * rows)

    @pl.when(s == steps - 1)
    def _():
        send(rows, 3 * rows)

    keep = jnp.where(t == 0, 0.0, 1.0)
    part = 256
    for p in range(hidden // part):
        pc = pl.ds(p * part, part)
        gate_i, gate_f, gate_g, gate_o = (gates_ref[:, pl.ds(k * hidden + p * part, part)] for k in range(4))
        tanh_c = jnp.tanh(c_ref[:, pc])
        c_prev = cp_ref[:, pc] * keep
        dh = e_ref[:, pc] + r_buf[:, pc]
        dc = dc_buf[:, pc] + dh * gate_o * (1.0 - tanh_c * tanh_c)
        dz = (
            dc * gate_g * gate_i * (1.0 - gate_i),
            dc * c_prev * gate_f * (1.0 - gate_f),
            dc * gate_i * (1.0 - gate_g * gate_g),
            dh * tanh_c * gate_o * (1.0 - gate_o),
        )
        dc_buf[:, pc] = dc * gate_f
        for k in range(4):
            cols = pl.ds(k * hidden + p * part, part)
            dz_buf[pl.ds(pl.multiple_of(t * rows, rows), rows), cols] = dz[k].astype(jnp.bfloat16)
            db_buf[:, cols] += jnp.sum(dz[k], axis=0, keepdims=True)

    @pl.when(s < steps - 1)
    def _():
        low = dz_buf[pl.ds(pl.multiple_of(t * rows, rows), rows), :]
        for p in range(hidden // part):
            pc = pl.ds(p * part, part)
            r_buf[:, pc] = lax.dot_general(low, w_rec[pc, :], NT, preferred_element_type=jnp.float32)

    @pl.when(s == steps - 1)
    def _():
        dz_buf[pl.ds(n, EXTRA), :] = jnp.broadcast_to(db_buf[...], (EXTRA, width)).astype(jnp.bfloat16)
        in_copy.wait()

        def dx_tile(p):
            pc = pl.ds(pl.multiple_of(p * part, part), part)
            dx_ref[:, pc] = lax.dot_general(dz_buf[pl.ds(0, n), :], w_in[pc, :], NT, preferred_element_type=jnp.float32)

        @pl.loop(0, 1)
        def _(p):
            dx_tile(p)

        send(0, rows)
        send(n, EXTRA)

        @pl.loop(1, hidden // part)
        def _(p):
            dx_tile(p)

        own_copy(0, n + EXTRA).wait()
        for k in range(1, PEERS):
            send_copy(k, 0, n + EXTRA).wait_send()
            cols = pl.ds(pl.multiple_of((chip * 2 + core) * share, share), share)
            pltpu.make_async_remote_copy(
                src_ref=dz_buf.at[:, cols],
                dst_ref=land.at[chips[k % 4] + 4 * (k // 4)],
                send_sem=send_sem.at[k],
                recv_sem=recv_sem.at[k],
                device_id=(chips[k % 4], cores[k // 4]),
                device_id_type=MESH,
            ).wait_recv()


def backward(layer, e_seq, gates, c_seq, w_stack, steps):
    n, hidden = e_seq.shape
    width = 4 * hidden
    rows = n // steps
    last = steps - 1
    anywhere = pl.BlockSpec(memory_space=pl.ANY)
    return pl.pallas_call(
        functools.partial(backward_kernel, layer, steps, rows, hidden),
        grid=(steps,),
        in_specs=[
            pl.BlockSpec((rows, hidden), lambda s: (last - s, 0)),
            pl.BlockSpec((rows, width), lambda s: (last - s, 0)),
            pl.BlockSpec((rows, hidden), lambda s: (last - s, 0)),
            pl.BlockSpec((rows, hidden), lambda s: (jnp.maximum(last - 1 - s, 0), 0)),
            anywhere,
        ],
        out_specs=[anywhere, pl.BlockSpec((n, hidden), lambda s: (0, 0))],
        out_shape=[
            jax.ShapeDtypeStruct((PEERS, n + EXTRA, width // PEERS), jnp.bfloat16),
            jax.ShapeDtypeStruct((n, hidden), jnp.float32),
        ],
        scratch_shapes=[
            pltpu.VMEM((rows, hidden), jnp.float32),
            pltpu.VMEM((rows, hidden), jnp.float32),
            pltpu.VMEM((1, width), jnp.float32),
            pltpu.VMEM((n + EXTRA, width), jnp.bfloat16),
            pltpu.VMEM((hidden, width), jnp.bfloat16),
            pltpu.VMEM((hidden, width), jnp.bfloat16),
            pltpu.SemaphoreType.DMA((2,)),
            pltpu.SemaphoreType.DMA,
            pltpu.SemaphoreType.DMA((PEERS,)),
            pltpu.SemaphoreType.DMA((PEERS,)),
        ],
        compiler_params=pltpu.CompilerParams(vmem_limit_bytes=VMEM_LIMIT, collective_id=layer, has_side_effects=True),
        cost_estimate=pl.CostEstimate(flops=2 * n * 2 * hidden * width * 4, bytes_accessed=2 * 2 * hidden * width, transcendentals=0),
        name="lstm_backward",
    )(e_seq, gates, c_seq, c_seq, w_stack)


def weight_kernel(n, rows, hidden, land_ref, u_own, u_other, h_own, h_other, out_ref, acc, db_acc, dz_t, dz_shift):
    s = pl.program_id(0)
    share = land_ref.shape[-1]

    @pl.when(s == 0)
    def _():
        acc[...] = jnp.zeros_like(acc)
        db_acc[...] = jnp.zeros_like(db_acc)

    db_acc[...] += land_ref[0, pl.ds(n, EXTRA), :].astype(jnp.float32)
    dz_t[...] = land_ref[0, pl.ds(0, n), :].T
    dz_shift[...] = jnp.concatenate([land_ref[0, pl.ds(rows, n - rows), :], jnp.zeros((rows, share), jnp.bfloat16)], axis=0).T
    part = 256

    def add(u_ref, h_ref):
        @pl.loop(0, hidden // part)
        def _(p):
            for base, lhs, rhs in ((0, dz_t, u_ref), (hidden, dz_shift, h_ref)):
                cols = pl.ds(pl.multiple_of(base + p * part, part), part)
                rc = pl.ds(pl.multiple_of(p * part, part), part)
                dw = jnp.dot(lhs[...], rhs[0, :, rc], preferred_element_type=jnp.float32)
                acc[:, cols] += dw.astype(jnp.bfloat16).astype(jnp.float32)

    @pl.when(s < CHIPS)
    def _():
        add(u_own, h_own)

    @pl.when(s >= CHIPS)
    def _():
        add(u_other, h_other)

    @pl.when(s == PEERS - 1)
    def _():
        @pl.loop(0, 2 * hidden // part)
        def _(p):
            cols = pl.ds(pl.multiple_of(p * part, part), part)
            out_ref[cols, :] = acc[:, cols].T.astype(jnp.bfloat16)

        out_ref[pl.ds(2 * hidden, EXTRA), :] = db_acc[...].astype(jnp.bfloat16)


def weight_gradient(land, u_all, h_all, rows):
    _, height, share = land.shape
    _, n, hidden = u_all[0].shape
    own = pl.BlockSpec((1, n, hidden), lambda s: (jnp.minimum(s, CHIPS - 1), 0, 0))
    other = pl.BlockSpec((1, n, hidden), lambda s: (jnp.maximum(s - CHIPS, 0), 0, 0))
    return pl.pallas_call(
        functools.partial(weight_kernel, n, rows, hidden),
        grid=(PEERS,),
        in_specs=[pl.BlockSpec((1, height, share), lambda s: (s, 0, 0)), own, other, own, other],
        out_specs=pl.BlockSpec((2 * hidden + EXTRA, share), lambda s: (0, 0)),
        out_shape=jax.ShapeDtypeStruct((2 * hidden + EXTRA, share), jnp.bfloat16),
        scratch_shapes=[
            pltpu.VMEM((share, 2 * hidden), jnp.float32),
            pltpu.VMEM((EXTRA, share), jnp.float32),
            pltpu.VMEM((share, n), jnp.bfloat16),
            pltpu.VMEM((share, n), jnp.bfloat16),
        ],
        compiler_params=pltpu.CompilerParams(vmem_limit_bytes=VMEM_LIMIT),
        cost_estimate=pl.CostEstimate(flops=2 * PEERS * n * share * 2 * hidden * 4, bytes_accessed=4 * PEERS * n * hidden, transcendentals=0),
        name="weight_gradient",
    )(land, *u_all, *h_all)


def cast_kernel(core_ref, own_ref, other_ref, own_db, other_db, *refs):
    out_ref, db_ref = refs[-2:]
    core = core_ref[0]
    share = own_ref.shape[-1]
    for chip in range(CHIPS):
        for which, src, src_db in ((core, own_ref, own_db), (1 - core, other_ref, other_db)):
            cols = pl.ds(pl.multiple_of((chip * 2 + which) * share, share), share)
            out_ref[0, :, cols] = src[chip].astype(jnp.float32)
            db_ref[0, :, cols] = src_db[chip, pl.ds(0, 8), :][0:1].astype(jnp.float32)


def cast_into(bufs, core, parts, layer, layers):
    own, other = parts
    _, height, share = own.shape
    height -= EXTRA
    tile = 128
    width = PEERS * share
    big = pl.BlockSpec((CHIPS, tile, share), lambda i: (0, i, 0))
    small = pl.BlockSpec((CHIPS, EXTRA, share), lambda i: (0, height // EXTRA, 0))
    return pl.pallas_call(
        cast_kernel,
        grid=(height // tile,),
        in_specs=[pl.BlockSpec(memory_space=pltpu.SMEM), big, big, small, small] + [pl.BlockSpec(memory_space=pl.ANY)] * len(bufs),
        out_specs=[pl.BlockSpec((1, tile, width), lambda i: (layer, i, 0)), pl.BlockSpec((1, 1, width), lambda i: (layer, 0, 0))],
        out_shape=[jax.ShapeDtypeStruct((layers, height, width), jnp.float32), jax.ShapeDtypeStruct((layers, 1, width), jnp.float32)],
        input_output_aliases={5: 0, 6: 1} if bufs else {},
        compiler_params=pltpu.CompilerParams(vmem_limit_bytes=VMEM_LIMIT),
        cost_estimate=pl.CostEstimate(flops=height * width * 100, bytes_accessed=6 * height * width, transcendentals=0),
        name="cast_gradient",
    )(core, own, other, own, other, *bufs)


def solution(mesh):
    batch_axes = ('replica', 'data')
    swap = [(0, 1), (1, 0)]

    def gather(part):
        own = lax.all_gather(part, 'replica')
        return own, lax.ppermute(own, 'data', swap)

    def local_grads(x_loc, dy_loc, w_stack, b_stack):
        layers = w_stack.shape[0]
        rows, steps, hidden = x_loc.shape
        n = rows * steps
        core = lax.axis_index('data').astype(jnp.int32).reshape(1)
        u = jnp.swapaxes(x_loc, 0, 1).reshape(n, hidden)
        b_rows = b_stack[:, None, :]
        gathered = [gather(u)]
        saved = []
        for layer in range(layers):
            gates, c_seq, u = forward(layer, u, w_stack, b_rows, steps)
            saved.append((gates, c_seq))
            gathered.append(gather(u))
        e_seq = jnp.swapaxes(dy_loc, 0, 1).reshape(n, hidden)
        bufs = ()
        pending = None
        for layer in reversed(range(layers)):
            land, e_seq = backward(layer, e_seq, *saved[layer], w_stack, steps)
            part = weight_gradient(land, gathered[layer], gathered[layer + 1], rows)
            part, e_seq = lax.optimization_barrier((part, e_seq))
            if pending is not None:
                part, pending = lax.optimization_barrier((part, pending))
            parts = gather(part)
            if pending is not None:
                bufs = cast_into(bufs, core, pending, layer + 1, layers)
            pending = parts
        dw, db = cast_into(bufs, core, pending, 0, layers)
        return dw, db.reshape(layers, 4 * hidden), jnp.swapaxes(e_seq.reshape(steps, rows, hidden), 0, 1)

    return jax.shard_map(local_grads, mesh=mesh, in_specs=(P(batch_axes), P(batch_axes), P(), P()), out_specs=(P(), P(), P(batch_axes)), check_vma=False)
```

time: 3070 us -> 1730 us (0.56)
  matrix products: 1250 us -> 0 us
  Pallas kernels: 0 us -> 863 us
  other arithmetic: 562 us -> 0 us
  local copies, waits for them, and re-layouts: 240 us -> 14.3 us
  waiting for transfers between devices: 945 us -> 835 us
    dot_general x216 -> x0, matrix products: 1250 us -> none  [the longest x96 572 us: time_step(): jnp.einsum('bg,hg->bh', dz_low, w_rec, preferred_element_type=jnp.float32)]
    pallas_call x0 -> x24, Pallas kernels: none -> 863 us  [the longest x6 399 us: backward(): pl.pallas_call(functools.partial(backward_kernel, layer, steps, rows, hid...]
    psum x1 -> x0, waiting for transfers between devices: 845 us -> none  [reduce_weights(): shard_sum = lax.psum(shard_sum, 'replica')]
    all_gather x6 -> x13, waiting for transfers between devices: 72.1 us -> 831 us  [gather(): own = lax.all_gather(part, 'replica')]
    concatenate x198 -> x0, other arithmetic: 268 us -> none  [the longest x192 224 us: time_step(): jnp.concatenate([dc_cur * gate_g * gate_i * (1.0 - gate_i), dc_cur * c_pr...]
    dynamic_update_slice x288 -> x0, other arithmetic: 193 us -> none  [the longest x192 123 us: layer_forward(): return lax.scan(time_step, init_state, in_proj)[1]]
    another operation x2 -> x0, other arithmetic: 95.9 us -> none  [the longest x1 95.3 us: local_grads(): jnp.stack(dw_list[::-1])]
    another operation x68 -> x0, local copies, waits for them, and re-layouts: 82.7 us -> none
  transfers between devices with their start and end apart: 13 -> 26, of which waited for: 7 -> 13; matrix products, arithmetic and copies ran while one was open for 33% -> 0% of each run, Pallas kernels for 0% -> 36%
where the time goes in v1:
time: 1730 us
  Pallas kernels  863 us (50%)
  waiting for transfers between devices  835 us (48%)
    all_gather x13, waiting for transfers between devices, gather(): own = lax.all_gather(part, 'replica')  831 us
    pallas_call x6, Pallas kernels, backward(): pl.pallas_call(functools.partial(backward_kernel, layer, steps, rows, hid...  399 us
    pallas_call x6, Pallas kernels, forward(): pl.pallas_call(functools.partial(forward_kernel, layer, steps, n // steps...  203 us
    pallas_call x6, Pallas kernels, weight_gradient(): pl.pallas_call(functools.partial(weight_kernel, n, rows, hidden), grid=(P...  147 us
    pallas_call x6, Pallas kernels, cast_into(): pl.pallas_call(cast_kernel, grid=(height // tile,), in_specs=[pl.BlockSpe...  115 us
  transfers between devices with their start and end apart: 26, of which 13 were waited for; matrix products, arithmetic and copies ran while one was open for 0% of the time, Pallas kernels for 36%

profile of v1, /device:TPU:0, one launch (start us, length us, event | category | flops | bytes accessed | tf_op | source)
XLA Modules:
  0.0 1727.1 jit_solution(15680981913121934211)
XLA Ops:
  11.6 33.9 %lstm_forward.6 = (f32[512,4096]{1,0:T(8,128)}, f32[512,1024]{1,0:T(8,128)}, bf16[512,1024]{1,0:T(8,128)(2,1)}) custom-call(bf16[512,1024]{1,0:T(8,128)(2,1)} %bitcast.43, bf16[6,2048,4096]{2,1,0:T(8,128)(2,1)} %w_hbm.23, f32[6,1,4096]{2,1,0:T(1,128)} %broadcast_in_dim.3.b_ref), custom_call_target="tpu_custom_call" | custom-call | flops 34359738368 | bytes 16777216 | tf_op jit(solution)/shard_map/lstm_forward/pallas_call | solution.py:87
  45.5 33.8 %lstm_forward.7 = (f32[512,4096]{1,0:T(8,128)}, f32[512,1024]{1,0:T(8,128)}, bf16[512,1024]{1,0:T(8,128)(2,1)}) custom-call(bf16[512,1024]{1,0:T(8,128)(2,1)} %get-tuple-element.72.u_ref, bf16[6,2048,4096]{2,1,0:T(8,128)(2,1)} %w_hbm.23, f32[6,1,4096]{2,1,0:T(1,128)} %broadcast_in_dim.3.b_ref), custom_call_target="tpu_custom_call" | custom-call | flops 34359738368 | bytes 16777216 | tf_op jit(solution)/shard_map/lstm_forward/pallas_call | solution.py:87
  79.3 33.8 %lstm_forward.8 = (f32[512,4096]{1,0:T(8,128)}, f32[512,1024]{1,0:T(8,128)}, bf16[512,1024]{1,0:T(8,128)(2,1)}) custom-call(bf16[512,1024]{1,0:T(8,128)(2,1)} %get-tuple-element.73.u_ref, bf16[6,2048,4096]{2,1,0:T(8,128)(2,1)} %w_hbm.23, f32[6,1,4096]{2,1,0:T(1,128)} %broadcast_in_dim.3.b_ref), custom_call_target="tpu_custom_call" | custom-call | flops 34359738368 | bytes 16777216 | tf_op jit(solution)/shard_map/lstm_forward/pallas_call | solution.py:87
  146.9 33.8 %lstm_forward.10 = (f32[512,4096]{1,0:T(8,128)}, f32[512,1024]{1,0:T(8,128)}, bf16[512,1024]{1,0:T(8,128)(2,1)}) custom-call(bf16[512,1024]{1,0:T(8,128)(2,1)} %get-tuple-element.75.u_ref, bf16[6,2048,4096]{2,1,0:T(8,128)(2,1)} %w_hbm.23, f32[6,1,4096]{2,1,0:T(1,128)} %broadcast_in_dim.3.b_ref), custom_call_target="tpu_custom_call" | custom-call | flops 34359738368 | bytes 16777216 | tf_op jit(solution)/shard_map/lstm_forward/pallas_call | solution.py:87
  180.7 33.8 %lstm_forward.11 = (f32[512,4096]{1,0:T(8,128)}, f32[512,1024]{1,0:T(8,128)}, bf16[512,1024]{1,0:T(8,128)(2,1)}) custom-call(bf16[512,1024]{1,0:T(8,128)(2,1)} %get-tuple-element.76.u_ref, bf16[6,2048,4096]{2,1,0:T(8,128)(2,1)} %w_hbm.23, f32[6,1,4096]{2,1,0:T(1,128)} %broadcast_in_dim.3.b_ref), custom_call_target="tpu_custom_call" | custom-call | flops 34359738368 | bytes 16777216 | tf_op jit(solution)/shard_map/lstm_forward/pallas_call | solution.py:87
  215.3 48.8 %all-gather.30.cloned.1.call-done = bf16[2048,1024]{1,0:T(8,128)(2,1)} async-done(((bf16[512,1024]{1,0:T(8,128)(2,1)}), bf16[2048,1024]{1,0:T(8,128)(2,1)}) %all-gather.30.cloned.1.call-update) | async-done | bytes 4194320 | tf_op jit(solution)/shard_map/all_gather | solution.py:375
  264.2 49.0 %all-gather.28.cloned.1.call-done = bf16[2048,1024]{1,0:T(8,128)(2,1)} async-done(((bf16[512,1024]{1,0:T(8,128)(2,1)}), bf16[2048,1024]{1,0:T(8,128)(2,1)}) %all-gather.28.cloned.1.call-update) | async-done | bytes 4194320 | tf_op jit(solution)/shard_map/all_gather | solution.py:375
  317.3 66.4 %lstm_backward.6 = (bf16[8,528,512]{2,1,0:T(8,128)(2,1)}, f32[512,1024]{1,0:T(8,128)}) custom-call(f32[512,1024]{1,0:T(8,128)} %bitcast.48, f32[512,4096]{1,0:T(8,128)} %get-tuple-element.77.gates_ref, f32[512,1024]{1,0:T(8,128)} %get-tuple-element.78.c_ref.cp_ref, f32[512,1024]{1,0:T(8,128)} %get-tuple-element.78.c_ref.cp_ref, bf16[6,2048,4096]{2,1,0:T(8,128)(2,1)} %w_hbm.23), custom_call_target="tpu_custom_call" | custom-call | flops 34359738368 | bytes 16777216 | tf_op jit(solution)/shard_map/lstm_backward/pallas_call | solution.py:241
  408.9 81.9 %all-gather.40.cloned.1.call-done = bf16[8256,512]{1,0:T(8,128)(2,1)} async-done(((bf16[2064,512]{1,0:T(8,128)(2,1)}), bf16[8256,512]{1,0:T(8,128)(2,1)}) %all-gather.40.cloned.1.call-update) | async-done | bytes 8454160 | tf_op jit(solution)/shard_map/all_gather | solution.py:375
  490.7 48.3 %all-gather.32.cloned.1.call-done = bf16[2048,1024]{1,0:T(8,128)(2,1)} async-done(((bf16[512,1024]{1,0:T(8,128)(2,1)}), bf16[2048,1024]{1,0:T(8,128)(2,1)}) %all-gather.32.cloned.1.call-update) | async-done | bytes 4194320 | tf_op jit(solution)/shard_map/all_gather | solution.py:375
  539.0 66.5 %lstm_backward.7 = (bf16[8,528,512]{2,1,0:T(8,128)(2,1)}, f32[512,1024]{1,0:T(8,128)}) custom-call(f32[512,1024]{1,0:T(8,128)} %get-tuple-element.82.e_ref, f32[512,4096]{1,0:T(8,128)} %get-tuple-element.83.gates_ref, f32[512,1024]{1,0:T(8,128)} %get-tuple-element.84.c_ref.cp_ref, f32[512,1024]{1,0:T(8,128)} %get-tuple-element.84.c_ref.cp_ref, ...), custom_call_target="tpu_custom_call" | custom-call | flops 34359738368 | bytes 16777216 | tf_op jit(solution)/shard_map/lstm_backward/pallas_call | solution.py:241
  630.7 81.9 %all-gather.42.cloned.1.call-done = bf16[8256,512]{1,0:T(8,128)(2,1)} async-done(((bf16[2064,512]{1,0:T(8,128)(2,1)}), bf16[8256,512]{1,0:T(8,128)(2,1)}) %all-gather.42.cloned.1.call-update) | async-done | bytes 8454160 | tf_op jit(solution)/shard_map/all_gather | solution.py:375
  712.6 48.3 %all-gather.34.cloned.1.call-done = bf16[2048,1024]{1,0:T(8,128)(2,1)} async-done(((bf16[512,1024]{1,0:T(8,128)(2,1)}), bf16[2048,1024]{1,0:T(8,128)(2,1)}) %all-gather.34.cloned.1.call-update) | async-done | bytes 4194320 | tf_op jit(solution)/shard_map/all_gather | solution.py:375
  760.9 66.3 %lstm_backward.8 = (bf16[8,528,512]{2,1,0:T(8,128)(2,1)}, f32[512,1024]{1,0:T(8,128)}) custom-call(f32[512,1024]{1,0:T(8,128)} %get-tuple-element.87.e_ref, f32[512,4096]{1,0:T(8,128)} %get-tuple-element.88.gates_ref, f32[512,1024]{1,0:T(8,128)} %get-tuple-element.89.c_ref.cp_ref, f32[512,1024]{1,0:T(8,128)} %get-tuple-element.89.c_ref.cp_ref, ...), custom_call_target="tpu_custom_call" | custom-call | flops 34359738368 | bytes 16777216 | tf_op jit(solution)/shard_map/lstm_backward/pallas_call | solution.py:241
  852.5 81.7 %all-gather.44.cloned.1.call-done = bf16[8256,512]{1,0:T(8,128)(2,1)} async-done(((bf16[2064,512]{1,0:T(8,128)(2,1)}), bf16[8256,512]{1,0:T(8,128)(2,1)}) %all-gather.44.cloned.1.call-update) | async-done | bytes 8454160 | tf_op jit(solution)/shard_map/all_gather | solution.py:375
  934.2 48.4 %all-gather.36.cloned.1.call-done = bf16[2048,1024]{1,0:T(8,128)(2,1)} async-done(((bf16[512,1024]{1,0:T(8,128)(2,1)}), bf16[2048,1024]{1,0:T(8,128)(2,1)}) %all-gather.36.cloned.1.call-update) | async-done | bytes 4194320 | tf_op jit(solution)/shard_map/all_gather | solution.py:375
  982.7 66.6 %lstm_backward.9 = (bf16[8,528,512]{2,1,0:T(8,128)(2,1)}, f32[512,1024]{1,0:T(8,128)}) custom-call(f32[512,1024]{1,0:T(8,128)} %get-tuple-element.92.e_ref, f32[512,4096]{1,0:T(8,128)} %get-tuple-element.93.gates_ref, f32[512,1024]{1,0:T(8,128)} %get-tuple-element.94.c_ref.cp_ref, f32[512,1024]{1,0:T(8,128)} %get-tuple-element.94.c_ref.cp_ref, ...), custom_call_target="tpu_custom_call" | custom-call | flops 34359738368 | bytes 16777216 | tf_op jit(solution)/shard_map/lstm_backward/pallas_call | solution.py:241
  1074.4 81.9 %all-gather.46.cloned.1.call-done = bf16[8256,512]{1,0:T(8,128)(2,1)} async-done(((bf16[2064,512]{1,0:T(8,128)(2,1)}), bf16[8256,512]{1,0:T(8,128)(2,1)}) %all-gather.46.cloned.1.call-update) | async-done | bytes 8454160 | tf_op jit(solution)/shard_map/all_gather | solution.py:375
  1156.3 48.3 %all-gather.38.cloned.1.call-done = bf16[2048,1024]{1,0:T(8,128)(2,1)} async-done(((bf16[512,1024]{1,0:T(8,128)(2,1)}), bf16[2048,1024]{1,0:T(8,128)(2,1)}) %all-gather.38.cloned.1.call-update) | async-done | bytes 4194320 | tf_op jit(solution)/shard_map/all_gather | solution.py:375
  1204.6 66.4 %lstm_backward.10 = (bf16[8,528,512]{2,1,0:T(8,128)(2,1)}, f32[512,1024]{1,0:T(8,128)}) custom-call(f32[512,1024]{1,0:T(8,128)} %get-tuple-element.97.e_ref, f32[512,4096]{1,0:T(8,128)} %get-tuple-element.98.gates_ref, f32[512,1024]{1,0:T(8,128)} %get-tuple-element.99.c_ref.cp_ref, f32[512,1024]{1,0:T(8,128)} %get-tuple-element.99.c_ref.cp_ref, ...), custom_call_target="tpu_custom_call" | custom-call | flops 34359738368 | bytes 16777216 | tf_op jit(solution)/shard_map/lstm_backward/pallas_call | solution.py:241
  1296.1 81.9 %all-gather.48.cloned.1.call-done = bf16[8256,512]{1,0:T(8,128)(2,1)} async-done(((bf16[2064,512]{1,0:T(8,128)(2,1)}), bf16[8256,512]{1,0:T(8,128)(2,1)}) %all-gather.48.cloned.1.call-update) | async-done | bytes 8454160 | tf_op jit(solution)/shard_map/all_gather | solution.py:375
  1378.0 48.3 %all-gather.26.cloned.1.call-done.u_own = bf16[4,512,1024]{2,1,0:T(8,128)(2,1)} async-done(((bf16[1,512,1024]{2,1,0:T(8,128)(2,1)}), bf16[4,512,1024]{2,1,0:T(8,128)(2,1)}) %all-gather.26.cloned.1.call-update) | async-done | bytes 4194320 | tf_op jit(solution)/shard_map/all_gather | solution.py:375
  1426.3 66.6 %lstm_backward.11 = (bf16[8,528,512]{2,1,0:T(8,128)(2,1)}, f32[512,1024]{1,0:T(8,128)}) custom-call(f32[512,1024]{1,0:T(8,128)} %get-tuple-element.102.e_ref, f32[512,4096]{1,0:T(8,128)} %get-tuple-element.103.gates_ref, f32[512,1024]{1,0:T(8,128)} %get-tuple-element.104.c_ref.cp_ref, f32[512,1024]{1,0:T(8,128)} %get-tuple-element.104.c_ref.cp_ref, ...), custom_call_target="tpu_custom_call" | custom-call | flops 34359738368 | bytes 16777216 | tf_op jit(solution)/shard_map/lstm_backward/pallas_call | solution.py:241
  1517.5 82.5 %all-gather.50.cloned.1.call-done = bf16[8256,512]{1,0:T(8,128)(2,1)} async-done(((bf16[2064,512]{1,0:T(8,128)(2,1)}), bf16[8256,512]{1,0:T(8,128)(2,1)}) %all-gather.50.cloned.1.call-update) | async-done | bytes 8454160 | tf_op jit(solution)/shard_map/all_gather | solution.py:375
  (70 shorter events, 313.7 us)
Async XLA Ops:
  7.2 257.0 %all-gather.30.cloned.1.call-start = ((), (), s32[]{:S(2)}) async-start(), calls=%async_computation.2 | async-start | bytes 5242880 | tf_op jit(solution)/shard_map/all_gather | solution.py:375
  214.5 98.7 %all-gather.28.cloned.1.call-start = ((), (), s32[]{:S(2)}) async-start(), calls=%async_computation.1 | async-start | bytes 5242880 | tf_op jit(solution)/shard_map/all_gather | solution.py:375
  215.3 275.5 %all-gather.40.cloned.1.call-start = ((), (), s32[]{:S(2)}) async-start(), calls=%async_computation.7 | async-start | bytes 10567680 | tf_op jit(solution)/shard_map/all_gather | solution.py:375
  264.1 119.5 %collective-permute-start.1 = (bf16[4,512,1024]{2,1,0:T(8,128)(2,1)}, bf16[4,512,1024]{2,1,0:T(8,128)(2,1)}, u32[]{:S(2)}, u32[]{:S(2)}) collective-permute-start(bf16[4,512,1024]{2,1,0:T(8,128)(2,1)} %bitcast.66), channel_id=1, source_target_pairs={{0,1},{1,0},{2,3},{3,2},{4,5},{5,4},{6,7},{7,6}} | collective-permute-start | bytes 12582920 | tf_op jit(solution)/shard_map/ppermute | solution.py:376
  313.2 70.5 %collective-permute-start = (bf16[4,512,1024]{2,1,0:T(8,128)(2,1)}, bf16[4,512,1024]{2,1,0:T(8,128)(2,1)}, u32[]{:S(2)}, u32[]{:S(2)}) collective-permute-start(bf16[4,512,1024]{2,1,0:T(8,128)(2,1)} %bitcast.54), channel_id=1, source_target_pairs={{0,1},{1,0},{2,3},{3,2},{4,5},{5,4},{6,7},{7,6}} | collective-permute-start | bytes 12582920 | tf_op jit(solution)/shard_map/ppermute | solution.py:376
  408.2 130.8 %all-gather.32.cloned.1.call-start = ((), (), s32[]{:S(2)}) async-start(), calls=%async_computation.3 | async-start | bytes 5242880 | tf_op jit(solution)/shard_map/all_gather | solution.py:375
  408.8 303.8 %all-gather.42.cloned.1.call-start = ((), (), s32[]{:S(2)}) async-start(), calls=%async_computation.8 | async-start | bytes 10567680 | tf_op jit(solution)/shard_map/all_gather | solution.py:375
  490.7 139.3 %collective-permute-start.7 = (bf16[4,2064,512]{2,1,0:T(8,128)(2,1)}, bf16[4,2064,512]{2,1,0:T(8,128)(2,1)}, u32[]{:S(2)}, u32[]{:S(2)}) collective-permute-start(bf16[4,2064,512]{2,1,0:T(8,128)(2,1)} %bitcast.40), channel_id=1, source_target_pairs={{0,1},{1,0},{2,3},{3,2},{4,5},{5,4},{6,7},{7,6}} | collective-permute-start | bytes 25362440 | tf_op jit(solution)/shard_map/ppermute | solution.py:376
  539.0 66.5 %collective-permute-start.2 = (bf16[4,512,1024]{2,1,0:T(8,128)(2,1)}, bf16[4,512,1024]{2,1,0:T(8,128)(2,1)}, u32[]{:S(2)}, u32[]{:S(2)}) collective-permute-start(bf16[4,512,1024]{2,1,0:T(8,128)(2,1)} %bitcast.57), channel_id=1, source_target_pairs={{0,1},{1,0},{2,3},{3,2},{4,5},{5,4},{6,7},{7,6}} | collective-permute-start | bytes 12582920 | tf_op jit(solution)/shard_map/ppermute | solution.py:376
  630.1 130.8 %all-gather.34.cloned.1.call-start = ((), (), s32[]{:S(2)}) async-start(), calls=%async_computation.4 | async-start | bytes 5242880 | tf_op jit(solution)/shard_map/all_gather | solution.py:375
  630.7 303.6 %all-gather.44.cloned.1.call-start = ((), (), s32[]{:S(2)}) async-start(), calls=%async_computation.9 | async-start | bytes 10567680 | tf_op jit(solution)/shard_map/all_gather | solution.py:375
  712.6 139.1 %collective-permute-start.8 = (bf16[4,2064,512]{2,1,0:T(8,128)(2,1)}, bf16[4,2064,512]{2,1,0:T(8,128)(2,1)}, u32[]{:S(2)}, u32[]{:S(2)}) collective-permute-start(bf16[4,2064,512]{2,1,0:T(8,128)(2,1)} %bitcast.25), channel_id=1, source_target_pairs={{0,1},{1,0},{2,3},{3,2},{4,5},{5,4},{6,7},{7,6}} | collective-permute-start | bytes 25362440 | tf_op jit(solution)/shard_map/ppermute | solution.py:376
  851.7 130.9 %all-gather.36.cloned.1.call-start = ((), (), s32[]{:S(2)}) async-start(), calls=%async_computation.5 | async-start | bytes 5242880 | tf_op jit(solution)/shard_map/all_gather | solution.py:375
  852.5 303.8 %all-gather.46.cloned.1.call-start = ((), (), s32[]{:S(2)}) async-start(), calls=%async_computation.10 | async-start | bytes 10567680 | tf_op jit(solution)/shard_map/all_gather | solution.py:375
  934.2 139.5 %collective-permute-start.9 = (bf16[4,2064,512]{2,1,0:T(8,128)(2,1)}, bf16[4,2064,512]{2,1,0:T(8,128)(2,1)}, u32[]{:S(2)}, u32[]{:S(2)}) collective-permute-start(bf16[4,2064,512]{2,1,0:T(8,128)(2,1)} %bitcast.28), channel_id=1, source_target_pairs={{0,1},{1,0},{2,3},{3,2},{4,5},{5,4},{6,7},{7,6}} | collective-permute-start | bytes 25362440 | tf_op jit(solution)/shard_map/ppermute | solution.py:376
  982.7 66.6 %collective-permute-start.4 = (bf16[4,512,1024]{2,1,0:T(8,128)(2,1)}, bf16[4,512,1024]{2,1,0:T(8,128)(2,1)}, u32[]{:S(2)}, u32[]{:S(2)}) collective-permute-start(bf16[4,512,1024]{2,1,0:T(8,128)(2,1)} %bitcast.63), channel_id=1, source_target_pairs={{0,1},{1,0},{2,3},{3,2},{4,5},{5,4},{6,7},{7,6}} | collective-permute-start | bytes 12582920 | tf_op jit(solution)/shard_map/ppermute | solution.py:376
  1073.8 130.8 %all-gather.38.cloned.1.call-start = ((), (), s32[]{:S(2)}) async-start(), calls=%async_computation.6 | async-start | bytes 5242880 | tf_op jit(solution)/shard_map/all_gather | solution.py:375
  1074.3 303.7 %all-gather.48.cloned.1.call-start = ((), (), s32[]{:S(2)}) async-start(), calls=%async_computation.11 | async-start | bytes 10567680 | tf_op jit(solution)/shard_map/all_gather | solution.py:375
  1156.3 139.2 %collective-permute-start.10 = (bf16[4,2064,512]{2,1,0:T(8,128)(2,1)}, bf16[4,2064,512]{2,1,0:T(8,128)(2,1)}, u32[]{:S(2)}, u32[]{:S(2)}) collective-permute-start(bf16[4,2064,512]{2,1,0:T(8,128)(2,1)} %bitcast.31), channel_id=1, source_target_pairs={{0,1},{1,0},{2,3},{3,2},{4,5},{5,4},{6,7},{7,6}} | collective-permute-start | bytes 25362440 | tf_op jit(solution)/shard_map/ppermute | solution.py:376
  1295.5 130.8 %all-gather.26.cloned.1.call-start = ((), (), s32[]{:S(2)}) async-start(), calls=%async_computation | async-start | bytes 5242880 | tf_op jit(solution)/shard_map/all_gather | solution.py:375
  1296.1 303.9 %all-gather.50.cloned.1.call-start = ((), (), s32[]{:S(2)}) async-start(), calls=%async_computation.12 | async-start | bytes 10567680 | tf_op jit(solution)/shard_map/all_gather | solution.py:375
  1378.0 139.4 %collective-permute-start.11 = (bf16[4,2064,512]{2,1,0:T(8,128)(2,1)}, bf16[4,2064,512]{2,1,0:T(8,128)(2,1)}, u32[]{:S(2)}, u32[]{:S(2)}) collective-permute-start(bf16[4,2064,512]{2,1,0:T(8,128)(2,1)} %bitcast.34), channel_id=1, source_target_pairs={{0,1},{1,0},{2,3},{3,2},{4,5},{5,4},{6,7},{7,6}} | collective-permute-start | bytes 25362440 | tf_op jit(solution)/shard_map/ppermute | solution.py:376
  1426.3 66.6 %collective-permute-start.6 = (bf16[4,512,1024]{2,1,0:T(8,128)(2,1)}, bf16[4,512,1024]{2,1,0:T(8,128)(2,1)}, u32[]{:S(2)}, u32[]{:S(2)}) collective-permute-start(bf16[4,512,1024]{2,1,0:T(8,128)(2,1)} %all-gather.26.cloned.1.call-done.u_own), channel_id=1, source_target_pairs={{0,1},{1,0},{2,3},{3,2},{4,5},{5,4},{6,7},{7,6}} | collective-permute-start | bytes 12582920 | tf_op jit(solution)/shard_map/ppermute | solution.py:376
  1600.0 99.6 %collective-permute-start.12 = (bf16[4,2064,512]{2,1,0:T(8,128)(2,1)}, bf16[4,2064,512]{2,1,0:T(8,128)(2,1)}, u32[]{:S(2)}, u32[]{:S(2)}) collective-permute-start(bf16[4,2064,512]{2,1,0:T(8,128)(2,1)} %bitcast.37), channel_id=1, source_target_pairs={{0,1},{1,0},{2,3},{3,2},{4,5},{5,4},{6,7},{7,6}} | collective-permute-start | bytes 25362440 | tf_op jit(solution)/shard_map/ppermute | solution.py:376
  (2 other events, 132.8 us)
Sparse Core Ops, SparseCore 0:
  214.6 49.4 all-gather.29
  266.5 46.6 all-gather.27
  408.4 82.3 all-gather.39
  492.4 46.6 all-gather.31
  630.2 82.3 all-gather.41
  714.2 46.6 all-gather.33
  851.8 82.3 all-gather.43
  936.0 46.6 all-gather.35
  1073.9 82.3 all-gather.45
  1157.9 46.6 all-gather.37
  1295.6 82.3 all-gather.47
  1379.6 46.6 all-gather.25
  1517.6 82.3 all-gather.49

commit v2 on v1

--- a/solution.py
+++ b/solution.py
@@ -112,7 +112,7 @@
     )(u, w_stack, b_stack)
 
 
-def backward_kernel(layer, steps, rows, hidden, e_ref, gates_ref, c_ref, cp_ref, w_hbm, land, dx_ref, r_buf, dc_buf, db_buf, dz_buf, w_in, w_rec, w_sem, own_sem, send_sem, recv_sem):
+def backward_kernel(layer, steps, rows, hidden, e_ref, gates_ref, c_ref, cp_ref, w_hbm, token_ref, land, dx_ref, r_buf, dc_buf, db_buf, dz_buf, w_in, w_rec, w_sem, own_sem, send_sem, recv_sem):
     s = pl.program_id(0)
     t = steps - 1 - s
     width = 4 * hidden
@@ -232,7 +232,7 @@
             ).wait_recv()
 
 
-def backward(layer, e_seq, gates, c_seq, w_stack, steps):
+def backward(layer, e_seq, gates, c_seq, w_stack, token, steps):
     n, hidden = e_seq.shape
     width = 4 * hidden
     rows = n // steps
@@ -247,6 +247,7 @@
             pl.BlockSpec((rows, hidden), lambda s: (last - s, 0)),
             pl.BlockSpec((rows, hidden), lambda s: (jnp.maximum(last - 1 - s, 0), 0)),
             anywhere,
+            anywhere,
         ],
         out_specs=[anywhere, pl.BlockSpec((n, hidden), lambda s: (0, 0))],
         out_shape=[
@@ -268,7 +269,7 @@
         compiler_params=pltpu.CompilerParams(vmem_limit_bytes=VMEM_LIMIT, collective_id=layer, has_side_effects=True),
         cost_estimate=pl.CostEstimate(flops=2 * n * 2 * hidden * width * 4, bytes_accessed=2 * 2 * hidden * width, transcendentals=0),
         name="lstm_backward",
-    )(e_seq, gates, c_seq, c_seq, w_stack)
+    )(e_seq, gates, c_seq, c_seq, w_stack, token)
 
 
 def weight_kernel(n, rows, hidden, land_ref, u_own, u_other, h_own, h_other, out_ref, acc, db_acc, dz_t, dz_shift):
@@ -336,7 +337,8 @@
 
 
 def cast_kernel(core_ref, own_ref, other_ref, own_db, other_db, *refs):
-    out_ref, db_ref = refs[-2:]
+    out_ref, db_ref, token_ref = refs[-3:]
+    token_ref[...] = jnp.zeros_like(token_ref)
     core = core_ref[0]
     share = own_ref.shape[-1]
     for chip in range(CHIPS):
@@ -358,8 +360,12 @@
         cast_kernel,
         grid=(height // tile,),
         in_specs=[pl.BlockSpec(memory_space=pltpu.SMEM), big, big, small, small] + [pl.BlockSpec(memory_space=pl.ANY)] * len(bufs),
-        out_specs=[pl.BlockSpec((1, tile, width), lambda i: (layer, i, 0)), pl.BlockSpec((1, 1, width), lambda i: (layer, 0, 0))],
-        out_shape=[jax.ShapeDtypeStruct((layers, height, width), jnp.float32), jax.ShapeDtypeStruct((layers, 1, width), jnp.float32)],
+        out_specs=[pl.BlockSpec((1, tile, width), lambda i: (layer, i, 0)), pl.BlockSpec((1, 1, width), lambda i: (layer, 0, 0)), pl.BlockSpec((8, 128), lambda i: (0, 0))],
+        out_shape=[
+            jax.ShapeDtypeStruct((layers, height, width), jnp.float32),
+            jax.ShapeDtypeStruct((layers, 1, width), jnp.float32),
+            jax.ShapeDtypeStruct((8, 128), jnp.float32),
+        ],
         input_output_aliases={5: 0, 6: 1} if bufs else {},
         compiler_params=pltpu.CompilerParams(vmem_limit_bytes=VMEM_LIMIT),
         cost_estimate=pl.CostEstimate(flops=height * width * 100, bytes_accessed=6 * height * width, transcendentals=0),
@@ -371,9 +377,8 @@
     batch_axes = ('replica', 'data')
     swap = [(0, 1), (1, 0)]
 
-    def gather(part):
-        own = lax.all_gather(part, 'replica')
-        return own, lax.ppermute(own, 'data', swap)
+    def tie(*values):
+        return lax.optimization_barrier(values)
 
     def local_grads(x_loc, dy_loc, w_stack, b_stack):
         layers = w_stack.shape[0]
@@ -382,26 +387,45 @@
         core = lax.axis_index('data').astype(jnp.int32).reshape(1)
         u = jnp.swapaxes(x_loc, 0, 1).reshape(n, hidden)
         b_rows = b_stack[:, None, :]
-        gathered = [gather(u)]
+        own = []
+        other = []
         saved = []
         for layer in range(layers):
+            own.append(lax.all_gather(u, 'replica'))
+            if layer >= 2:
+                u, own[layer - 2] = tie(u, own[layer - 2])
+                other.append(lax.ppermute(own[layer - 2], 'data', swap))
+            if layer >= 3:
+                u, other[layer - 3] = tie(u, other[layer - 3])
             gates, c_seq, u = forward(layer, u, w_stack, b_rows, steps)
             saved.append((gates, c_seq))
-            gathered.append(gather(u))
+        own.append(lax.all_gather(u, 'replica'))
         e_seq = jnp.swapaxes(dy_loc, 0, 1).reshape(n, hidden)
+        e_seq, own[layers - 2], other[layers - 3] = tie(e_seq, own[layers - 2], other[layers - 3])
+        other.append(lax.ppermute(own[layers - 2], 'data', swap))
         bufs = ()
-        pending = None
+        tokens = {}
+        start = jnp.zeros((8, 128), jnp.float32)
+        shard_own = None
         for layer in reversed(range(layers)):
-            land, e_seq = backward(layer, e_seq, *saved[layer], w_stack, steps)
-            part = weight_gradient(land, gathered[layer], gathered[layer + 1], rows)
-            part, e_seq = lax.optimization_barrier((part, e_seq))
-            if pending is not None:
-                part, pending = lax.optimization_barrier((part, pending))
-            parts = gather(part)
-            if pending is not None:
-                bufs = cast_into(bufs, core, pending, layer + 1, layers)
-            pending = parts
-        dw, db = cast_into(bufs, core, pending, 0, layers)
+            token = tokens.get(layer + 3, start)
+            land, e_seq = backward(layer, e_seq, *saved[layer], w_stack, token, steps)
+            if layer == layers - 1:
+                land, own[layers - 1], own[layers] = tie(land, own[layers - 1], own[layers])
+                other.append(lax.ppermute(own[layers - 1], 'data', swap))
+                other.append(lax.ppermute(own[layers], 'data', swap))
+            part = weight_gradient(land, (own[layer], other[layer]), (own[layer + 1], other[layer + 1]), rows)
+            part, e_seq = tie(part, e_seq)
+            if shard_own is not None:
+                part, shard_own = tie(part, shard_own)
+            next_own = lax.all_gather(part, 'replica')
+            if shard_own is not None:
+                shard_other = lax.ppermute(shard_own, 'data', swap)
+                *bufs, tokens[layer + 1] = cast_into(bufs, core, (shard_own, shard_other), layer + 1, layers)
+            shard_own = next_own
+        shard_own, bufs[1] = tie(shard_own, bufs[1])
+        shard_other = lax.ppermute(shard_own, 'data', swap)
+        dw, db, _ = cast_into(bufs, core, (shard_own, shard_other), 0, layers)
         return dw, db.reshape(layers, 4 * hidden), jnp.swapaxes(e_seq.reshape(steps, rows, hidden), 0, 1)
 
     return jax.shard_map(local_grads, mesh=mesh, in_specs=(P(batch_axes), P(batch_axes), P(), P()), out_specs=(P(), P(), P(batch_axes)), check_vma=False)

time: 1730 us -> 1280 us (0.74)
  waiting for transfers between devices: 835 us -> 174 us
  Pallas kernels: 863 us -> 1060 us
    all_gather x13, waiting for transfers between devices: 831 us -> 140 us  [the longest x7 81.3 us: local_grads(): own.append(lax.all_gather(u, 'replica'))]
    pallas_call x6, Pallas kernels: 399 us -> 595 us  [backward(): pl.pallas_call(functools.partial(backward_kernel, layer, steps, rows, hid...]
    ppermute x13, waiting for transfers between devices: 0.03 us -> 34.4 us  [the longest x6 21.8 us: local_grads(): shard_other = lax.ppermute(shard_own, 'data', swap)]
  transfers between devices with their start and end apart: 26 -> 26, of which waited for: 13 -> 11; matrix products, arithmetic and copies ran while one was open for 0% -> 1% of each run, Pallas kernels for 36% -> 80%
where the time goes in v2:
time: 1280 us; the launch traced here: 1270 us
  Pallas kernels  1060 us (83%)
  waiting for transfers between devices  174 us (14%)
  local copies, waits for them, and re-layouts  14.8 us (1%)
  between operations  14.5 us (1%)
    pallas_call x6, Pallas kernels, backward(): pl.pallas_call(functools.partial(backward_kernel, layer, steps, rows, hid...  595 us
    pallas_call x6, Pallas kernels, forward(): pl.pallas_call(functools.partial(forward_kernel, layer, steps, n // steps...  203 us
    pallas_call x6, Pallas kernels, weight_gradient(): pl.pallas_call(functools.partial(weight_kernel, n, rows, hidden), grid=(P...  147 us
    pallas_call x6, Pallas kernels, cast_into(): pl.pallas_call(cast_kernel, grid=(height // tile,), in_specs=[pl.BlockSpe...  115 us
    all_gather x7, waiting for transfers between devices, local_grads(): own.append(lax.all_gather(u, 'replica'))  81.3 us
    all_gather x6, waiting for transfers between devices, local_grads(): next_own = lax.all_gather(part, 'replica')  58.4 us
  transfers between devices with their start and end apart: 26, of which 11 were waited for; matrix products, arithmetic and copies ran while one was open for 1% of the time, Pallas kernels for 80%

profile of v2, /device:TPU:0, one launch (start us, length us, event | category | flops | bytes accessed | tf_op | source)
XLA Modules:
  0.0 1268.5 jit_solution(10101588333498524743)
XLA Ops:
  11.7 33.8 %lstm_forward.6 = (f32[512,4096]{1,0:T(8,128)}, f32[512,1024]{1,0:T(8,128)}, bf16[512,1024]{1,0:T(8,128)(2,1)}) custom-call(bf16[512,1024]{1,0:T(8,128)(2,1)} %bitcast.44, bf16[6,2048,4096]{2,1,0:T(8,128)(2,1)} %w_hbm.23, f32[6,1,4096]{2,1,0:T(1,128)} %broadcast_in_dim.6.b_ref), custom_call_target="tpu_custom_call" | custom-call | flops 34359738368 | bytes 16777216 | tf_op jit(solution)/shard_map/lstm_forward/pallas_call | solution.py:87
  45.5 33.8 %lstm_forward.7 = (f32[512,4096]{1,0:T(8,128)}, f32[512,1024]{1,0:T(8,128)}, bf16[512,1024]{1,0:T(8,128)(2,1)}) custom-call(bf16[512,1024]{1,0:T(8,128)(2,1)} %get-tuple-element.92.u_ref, bf16[6,2048,4096]{2,1,0:T(8,128)(2,1)} %w_hbm.23, f32[6,1,4096]{2,1,0:T(1,128)} %broadcast_in_dim.6.b_ref), custom_call_target="tpu_custom_call" | custom-call | flops 34359738368 | bytes 16777216 | tf_op jit(solution)/shard_map/lstm_forward/pallas_call | solution.py:87
  80.5 33.8 %lstm_forward.8 = (f32[512,4096]{1,0:T(8,128)}, f32[512,1024]{1,0:T(8,128)}, bf16[512,1024]{1,0:T(8,128)(2,1)}) custom-call(bf16[512,1024]{1,0:T(8,128)(2,1)} %get-tuple-element.94.u_ref, bf16[6,2048,4096]{2,1,0:T(8,128)(2,1)} %w_hbm.23, f32[6,1,4096]{2,1,0:T(1,128)} %broadcast_in_dim.6.b_ref), custom_call_target="tpu_custom_call" | custom-call | flops 34359738368 | bytes 16777216 | tf_op jit(solution)/shard_map/lstm_forward/pallas_call | solution.py:87
  114.5 33.8 %lstm_forward.9 = (f32[512,4096]{1,0:T(8,128)}, f32[512,1024]{1,0:T(8,128)}, bf16[512,1024]{1,0:T(8,128)(2,1)}) custom-call(bf16[512,1024]{1,0:T(8,128)(2,1)} %get-tuple-element.98.u_ref, bf16[6,2048,4096]{2,1,0:T(8,128)(2,1)} %w_hbm.23, f32[6,1,4096]{2,1,0:T(1,128)} %broadcast_in_dim.6.b_ref), custom_call_target="tpu_custom_call" | custom-call | flops 34359738368 | bytes 16777216 | tf_op jit(solution)/shard_map/lstm_forward/pallas_call | solution.py:87
  157.5 33.8 %lstm_forward.10 = (f32[512,4096]{1,0:T(8,128)}, f32[512,1024]{1,0:T(8,128)}, bf16[512,1024]{1,0:T(8,128)(2,1)}) custom-call(bf16[512,1024]{1,0:T(8,128)(2,1)} %get-tuple-element.102.u_ref, bf16[6,2048,4096]{2,1,0:T(8,128)(2,1)} %w_hbm.23, f32[6,1,4096]{2,1,0:T(1,128)} %broadcast_in_dim.6.b_ref), custom_call_target="tpu_custom_call" | custom-call | flops 34359738368 | bytes 16777216 | tf_op jit(solution)/shard_map/lstm_forward/pallas_call | solution.py:87
  206.4 33.8 %lstm_forward.11 = (f32[512,4096]{1,0:T(8,128)}, f32[512,1024]{1,0:T(8,128)}, bf16[512,1024]{1,0:T(8,128)(2,1)}) custom-call(bf16[512,1024]{1,0:T(8,128)(2,1)} %get-tuple-element.108.u_ref, bf16[6,2048,4096]{2,1,0:T(8,128)(2,1)} %w_hbm.23, f32[6,1,4096]{2,1,0:T(1,128)} %broadcast_in_dim.6.b_ref), custom_call_target="tpu_custom_call" | custom-call | flops 34359738368 | bytes 16777216 | tf_op jit(solution)/shard_map/lstm_forward/pallas_call | solution.py:87
  255.3 90.4 %lstm_backward.6 = (bf16[8,528,512]{2,1,0:T(8,128)(2,1)}, f32[512,1024]{1,0:T(8,128)}) custom-call(f32[512,1024]{1,0:T(8,128)} %bitcast.48, f32[512,4096]{1,0:T(8,128)} %get-tuple-element.109.gates_ref, f32[512,1024]{1,0:T(8,128)} %get-tuple-element.110.c_ref.cp_ref, f32[512,1024]{1,0:T(8,128)} %get-tuple-element.110.c_ref.cp_ref, ...), custom_call_target="tpu_custom_call" | custom-call | flops 34359738368 | bytes 16777216 | tf_op jit(solution)/shard_map/lstm_backward/pallas_call | solution.py:241
  345.7 47.6 %all-gather.38.cloned.1.call-done = bf16[2048,1024]{1,0:T(8,128)(2,1)} async-done(((bf16[512,1024]{1,0:T(8,128)(2,1)}), bf16[2048,1024]{1,0:T(8,128)(2,1)}) %all-gather.38.cloned.1.call-update) | async-done | bytes 4194320 | tf_op jit(solution)/shard_map/all_gather | solution.py:402
  406.3 24.4 %weight_gradient.6 = bf16[2064,512]{1,0:T(8,128)(2,1)} custom-call(bf16[8,528,512]{2,1,0:T(8,128)(2,1)} %get-tuple-element.113.land_ref, bf16[4,512,1024]{2,1,0:T(8,128)(2,1)} %bitcast.64, bf16[4,512,1024]{2,1,0:T(8,128)(2,1)} %collective-permute-done.4.u_other.h_other, bf16[4,512,1024]{2,1,0:T(8,128)(2,1)} %bitcast.67, ...), custom_call_target="tpu_custom_call" | custom-call | flops 34359738368 | bytes 16777216 | tf_op jit(solution)/shard_map/weight_gradient/pallas_call | solution.py:321
  431.3 88.4 %lstm_backward.7 = (bf16[8,528,512]{2,1,0:T(8,128)(2,1)}, f32[512,1024]{1,0:T(8,128)}) custom-call(f32[512,1024]{1,0:T(8,128)} %get-tuple-element.117.e_ref, f32[512,4096]{1,0:T(8,128)} %get-tuple-element.118.gates_ref, f32[512,1024]{1,0:T(8,128)} %get-tuple-element.119.c_ref.cp_ref, f32[512,1024]{1,0:T(8,128)} %get-tuple-element.119.c_ref.cp_ref, ...), custom_call_target="tpu_custom_call" | custom-call | flops 34359738368 | bytes 16777216 | tf_op jit(solution)/shard_map/lstm_backward/pallas_call | solution.py:241
  519.7 24.5 %weight_gradient.7 = bf16[2064,512]{1,0:T(8,128)(2,1)} custom-call(bf16[8,528,512]{2,1,0:T(8,128)(2,1)} %get-tuple-element.120.land_ref, bf16[4,512,1024]{2,1,0:T(8,128)(2,1)} %bitcast.61, bf16[4,512,1024]{2,1,0:T(8,128)(2,1)} %collective-permute-done.6.u_other.h_other, bf16[4,512,1024]{2,1,0:T(8,128)(2,1)} %bitcast.65, ...), custom_call_target="tpu_custom_call" | custom-call | flops 34359738368 | bytes 16777216 | tf_op jit(solution)/shard_map/weight_gradient/pallas_call | solution.py:321
  555.1 84.2 %lstm_backward.8 = (bf16[8,528,512]{2,1,0:T(8,128)(2,1)}, f32[512,1024]{1,0:T(8,128)}) custom-call(f32[512,1024]{1,0:T(8,128)} %get-tuple-element.123.e_ref, f32[512,4096]{1,0:T(8,128)} %get-tuple-element.124.gates_ref, f32[512,1024]{1,0:T(8,128)} %get-tuple-element.125.c_ref.cp_ref, f32[512,1024]{1,0:T(8,128)} %get-tuple-element.125.c_ref.cp_ref, ...), custom_call_target="tpu_custom_call" | custom-call | flops 34359738368 | bytes 16777216 | tf_op jit(solution)/shard_map/lstm_backward/pallas_call | solution.py:241
  640.0 24.4 %weight_gradient.8 = bf16[2064,512]{1,0:T(8,128)(2,1)} custom-call(bf16[8,528,512]{2,1,0:T(8,128)(2,1)} %get-tuple-element.126.land_ref, bf16[4,512,1024]{2,1,0:T(8,128)(2,1)} %bitcast.58, bf16[4,512,1024]{2,1,0:T(8,128)(2,1)} %collective-permute-done.2.u_other.h_other, bf16[4,512,1024]{2,1,0:T(8,128)(2,1)} %bitcast.62, ...), custom_call_target="tpu_custom_call" | custom-call | flops 34359738368 | bytes 16777216 | tf_op jit(solution)/shard_map/weight_gradient/pallas_call | solution.py:321
  681.1 19.1 %cast_gradient.6 = (f32[6,2048,4096]{2,1,0:T(8,128)}, f32[6,1,4096]{2,1,0:T(1,128)}, f32[8,128]{1,0:T(8,128)}) custom-call(s32[1]{0:T(128)} %bitcast.core_ref, bf16[4,2064,512]{2,1,0:T(8,128)(2,1)} %bitcast.41, bf16[4,2064,512]{2,1,0:T(8,128)(2,1)} %collective-permute-done.7.other_ref.other_db, bf16[4,2064,512]{2,1,0:T(8,128)(2,1)} %bitcast.42, ...), custom_call_target="tpu_custom_call" | custom-call | flops 838860800 | bytes 50331648 | tf_op jit(solution)/shard_map/cast_gradient/pallas_call | solution.py:359
  700.2 111.0 %lstm_backward.9 = (bf16[8,528,512]{2,1,0:T(8,128)(2,1)}, f32[512,1024]{1,0:T(8,128)}) custom-call(f32[512,1024]{1,0:T(8,128)} %get-tuple-element.129.e_ref, f32[512,4096]{1,0:T(8,128)} %get-tuple-element.130.gates_ref, f32[512,1024]{1,0:T(8,128)} %get-tuple-element.131.c_ref.cp_ref, f32[512,1024]{1,0:T(8,128)} %get-tuple-element.131.c_ref.cp_ref, ...), custom_call_target="tpu_custom_call" | custom-call | flops 34359738368 | bytes 16777216 | tf_op jit(solution)/shard_map/lstm_backward/pallas_call | solution.py:241
  811.6 24.5 %weight_gradient.9 = bf16[2064,512]{1,0:T(8,128)(2,1)} custom-call(bf16[8,528,512]{2,1,0:T(8,128)(2,1)} %get-tuple-element.136.land_ref, bf16[4,512,1024]{2,1,0:T(8,128)(2,1)} %bitcast.55, bf16[4,512,1024]{2,1,0:T(8,128)(2,1)} %collective-permute-done.3.u_other.h_other, bf16[4,512,1024]{2,1,0:T(8,128)(2,1)} %bitcast.59, ...), custom_call_target="tpu_custom_call" | custom-call | flops 34359738368 | bytes 16777216 | tf_op jit(solution)/shard_map/weight_gradient/pallas_call | solution.py:321
  836.1 19.1 %cast_gradient.7 = (f32[6,2048,4096]{2,1,0:T(8,128)}, f32[6,1,4096]{2,1,0:T(1,128)}, f32[8,128]{1,0:T(8,128)}) custom-call(s32[1]{0:T(128)} %bitcast.core_ref, bf16[4,2064,512]{2,1,0:T(8,128)(2,1)} %bitcast.32, bf16[4,2064,512]{2,1,0:T(8,128)(2,1)} %collective-permute-done.8.other_ref.other_db, ...), custom_call_target="tpu_custom_call", output_to_operand_aliasing={{0}: (5, {}), {1}: (6, {})} | custom-call | flops 838860800 | bytes 50331648 | tf_op jit(solution)/shard_map/cast_gradient/pallas_call | solution.py:359
  855.2 110.4 %lstm_backward.10 = (bf16[8,528,512]{2,1,0:T(8,128)(2,1)}, f32[512,1024]{1,0:T(8,128)}) custom-call(f32[512,1024]{1,0:T(8,128)} %get-tuple-element.139.e_ref, f32[512,4096]{1,0:T(8,128)} %get-tuple-element.140.gates_ref, f32[512,1024]{1,0:T(8,128)} %get-tuple-element.141.c_ref.cp_ref, f32[512,1024]{1,0:T(8,128)} %get-tuple-element.141.c_ref.cp_ref, ...), custom_call_target="tpu_custom_call" | custom-call | flops 34359738368 | bytes 16777216 | tf_op jit(solution)/shard_map/lstm_backward/pallas_call | solution.py:241
  965.9 24.5 %weight_gradient.10 = bf16[2064,512]{1,0:T(8,128)(2,1)} custom-call(bf16[8,528,512]{2,1,0:T(8,128)(2,1)} %get-tuple-element.148.land_ref, bf16[4,512,1024]{2,1,0:T(8,128)(2,1)} %bitcast.52, bf16[4,512,1024]{2,1,0:T(8,128)(2,1)} %collective-permute-done.1.u_other.h_other, bf16[4,512,1024]{2,1,0:T(8,128)(2,1)} %bitcast.56, ...), custom_call_target="tpu_custom_call" | custom-call | flops 34359738368 | bytes 16777216 | tf_op jit(solution)/shard_map/weight_gradient/pallas_call | solution.py:321
  990.7 19.1 %cast_gradient.8 = (f32[6,2048,4096]{2,1,0:T(8,128)}, f32[6,1,4096]{2,1,0:T(1,128)}, f32[8,128]{1,0:T(8,128)}) custom-call(s32[1]{0:T(128)} %bitcast.core_ref, bf16[4,2064,512]{2,1,0:T(8,128)(2,1)} %bitcast.29, bf16[4,2064,512]{2,1,0:T(8,128)(2,1)} %collective-permute-done.9.other_ref.other_db, ...), custom_call_target="tpu_custom_call", output_to_operand_aliasing={{0}: (5, {}), {1}: (6, {})} | custom-call | flops 838860800 | bytes 50331648 | tf_op jit(solution)/shard_map/cast_gradient/pallas_call | solution.py:359
  1009.8 110.6 %lstm_backward.11 = (bf16[8,528,512]{2,1,0:T(8,128)(2,1)}, f32[512,1024]{1,0:T(8,128)}) custom-call(f32[512,1024]{1,0:T(8,128)} %get-tuple-element.151.e_ref, f32[512,4096]{1,0:T(8,128)} %get-tuple-element.152.gates_ref, f32[512,1024]{1,0:T(8,128)} %get-tuple-element.153.c_ref.cp_ref, f32[512,1024]{1,0:T(8,128)} %get-tuple-element.153.c_ref.cp_ref, ...), custom_call_target="tpu_custom_call" | custom-call | flops 34359738368 | bytes 16777216 | tf_op jit(solution)/shard_map/lstm_backward/pallas_call | solution.py:241
  1120.5 24.6 %weight_gradient.11 = bf16[2064,512]{1,0:T(8,128)(2,1)} custom-call(bf16[8,528,512]{2,1,0:T(8,128)(2,1)} %get-tuple-element.160.land_ref, bf16[4,512,1024]{2,1,0:T(8,128)(2,1)} %all-gather.26.cloned.1.call-done.u_own, bf16[4,512,1024]{2,1,0:T(8,128)(2,1)} %collective-permute-done.u_other, bf16[4,512,1024]{2,1,0:T(8,128)(2,1)} %bitcast.53, ...), custom_call_target="tpu_custom_call" | custom-call | flops 34359738368 | bytes 16777216 | tf_op jit(solution)/shard_map/weight_gradient/pallas_call | solution.py:321
  1177.4 19.1 %cast_gradient.10 = (f32[6,2048,4096]{2,1,0:T(8,128)}, f32[6,1,4096]{2,1,0:T(1,128)}, f32[8,128]{1,0:T(8,128)}) custom-call(s32[1]{0:T(128)} %bitcast.core_ref, bf16[4,2064,512]{2,1,0:T(8,128)(2,1)} %bitcast.35, bf16[4,2064,512]{2,1,0:T(8,128)(2,1)} %collective-permute-done.10.other_ref.other_db, ...), custom_call_target="tpu_custom_call", output_to_operand_aliasing={{0}: (5, {}), {1}: (6, {})} | custom-call | flops 838860800 | bytes 50331648 | tf_op jit(solution)/shard_map/cast_gradient/pallas_call | solution.py:359
  1196.5 31.1 %all-gather.50.cloned.1.call-done = bf16[8256,512]{1,0:T(8,128)(2,1)} async-done(((bf16[2064,512]{1,0:T(8,128)(2,1)}), bf16[8256,512]{1,0:T(8,128)(2,1)}) %all-gather.50.cloned.1.call-update) | async-done | bytes 8454160 | tf_op jit(solution)/shard_map/all_gather | solution.py:421
  (71 shorter events, 154.1 us)
Async XLA Ops:
  7.2 72.5 %all-gather.26.cloned.1.call-start = ((), (), s32[]{:S(2)}) async-start(), calls=%async_computation | async-start | bytes 5242880 | tf_op jit(solution)/shard_map/all_gather | solution.py:394
  10.0 104.4 %all-gather.28.cloned.1.call-start = ((), (), s32[]{:S(2)}) async-start(), calls=%async_computation.1 | async-start | bytes 5242880 | tf_op jit(solution)/shard_map/all_gather | solution.py:394
  45.5 112.0 %all-gather.32.cloned.1.call-start = ((), (), s32[]{:S(2)}) async-start(), calls=%async_computation.3 | async-start | bytes 5242880 | tf_op jit(solution)/shard_map/all_gather | solution.py:394
  79.4 127.0 %all-gather.34.cloned.1.call-start = ((), (), s32[]{:S(2)}) async-start(), calls=%async_computation.4 | async-start | bytes 5242880 | tf_op jit(solution)/shard_map/all_gather | solution.py:394
  79.7 34.8 %collective-permute-start = (bf16[4,512,1024]{2,1,0:T(8,128)(2,1)}, bf16[4,512,1024]{2,1,0:T(8,128)(2,1)}, u32[]{:S(2)}, u32[]{:S(2)}) collective-permute-start(bf16[4,512,1024]{2,1,0:T(8,128)(2,1)} %all-gather.26.cloned.1.call-done.u_own), channel_id=1, source_target_pairs={{0,1},{1,0},{2,3},{3,2},{4,5},{5,4},{6,7},{7,6}} | collective-permute-start | bytes 12582920 | tf_op jit(solution)/shard_map/ppermute | solution.py:397
  114.4 140.3 %all-gather.30.cloned.1.call-start = ((), (), s32[]{:S(2)}) async-start(), calls=%async_computation.2 | async-start | bytes 5242880 | tf_op jit(solution)/shard_map/all_gather | solution.py:394
  114.4 43.1 %collective-permute-start.1 = (bf16[4,512,1024]{2,1,0:T(8,128)(2,1)}, bf16[4,512,1024]{2,1,0:T(8,128)(2,1)}, u32[]{:S(2)}, u32[]{:S(2)}) collective-permute-start(bf16[4,512,1024]{2,1,0:T(8,128)(2,1)} %bitcast.51), channel_id=1, source_target_pairs={{0,1},{1,0},{2,3},{3,2},{4,5},{5,4},{6,7},{7,6}} | collective-permute-start | bytes 12582920 | tf_op jit(solution)/shard_map/ppermute | solution.py:397
  148.3 197.4 %all-gather.36.cloned.1.call-start = ((), (), s32[]{:S(2)}) async-start(), calls=%async_computation.5 | async-start | bytes 5242880 | tf_op jit(solution)/shard_map/all_gather | solution.py:394
  157.5 48.9 %collective-permute-start.3 = (bf16[4,512,1024]{2,1,0:T(8,128)(2,1)}, bf16[4,512,1024]{2,1,0:T(8,128)(2,1)}, u32[]{:S(2)}, u32[]{:S(2)}) collective-permute-start(bf16[4,512,1024]{2,1,0:T(8,128)(2,1)} %bitcast.54), channel_id=1, source_target_pairs={{0,1},{1,0},{2,3},{3,2},{4,5},{5,4},{6,7},{7,6}} | collective-permute-start | bytes 12582920 | tf_op jit(solution)/shard_map/ppermute | solution.py:397
  191.3 201.9 %all-gather.38.cloned.1.call-start = ((), (), s32[]{:S(2)}) async-start(), calls=%async_computation.6 | async-start | bytes 5242880 | tf_op jit(solution)/shard_map/all_gather | solution.py:402
  206.4 48.3 %collective-permute-start.2 = (bf16[4,512,1024]{2,1,0:T(8,128)(2,1)}, bf16[4,512,1024]{2,1,0:T(8,128)(2,1)}, u32[]{:S(2)}, u32[]{:S(2)}) collective-permute-start(bf16[4,512,1024]{2,1,0:T(8,128)(2,1)} %bitcast.57), channel_id=1, source_target_pairs={{0,1},{1,0},{2,3},{3,2},{4,5},{5,4},{6,7},{7,6}} | collective-permute-start | bytes 12582920 | tf_op jit(solution)/shard_map/ppermute | solution.py:397
  240.2 314.8 %all-gather.40.cloned.1.call-start = ((), (), s32[]{:S(2)}) async-start(), calls=%async_computation.7 | async-start | bytes 10567680 | tf_op jit(solution)/shard_map/all_gather | solution.py:421
  430.8 250.0 %all-gather.42.cloned.1.call-start = ((), (), s32[]{:S(2)}) async-start(), calls=%async_computation.8 | async-start | bytes 10567680 | tf_op jit(solution)/shard_map/all_gather | solution.py:421
  431.0 88.7 %collective-permute-start.6 = (bf16[4,512,1024]{2,1,0:T(8,128)(2,1)}, bf16[4,512,1024]{2,1,0:T(8,128)(2,1)}, u32[]{:S(2)}, u32[]{:S(2)}) collective-permute-start(bf16[4,512,1024]{2,1,0:T(8,128)(2,1)} %bitcast.60), channel_id=1, source_target_pairs={{0,1},{1,0},{2,3},{3,2},{4,5},{5,4},{6,7},{7,6}} | collective-permute-start | bytes 12582920 | tf_op jit(solution)/shard_map/ppermute | solution.py:405
  555.1 280.9 %all-gather.44.cloned.1.call-start = ((), (), s32[]{:S(2)}) async-start(), calls=%async_computation.9 | async-start | bytes 10567680 | tf_op jit(solution)/shard_map/all_gather | solution.py:421
  639.3 41.8 %collective-permute-start.7 = (bf16[4,2064,512]{2,1,0:T(8,128)(2,1)}, bf16[4,2064,512]{2,1,0:T(8,128)(2,1)}, u32[]{:S(2)}, u32[]{:S(2)}) collective-permute-start(bf16[4,2064,512]{2,1,0:T(8,128)(2,1)} %bitcast.40), channel_id=1, source_target_pairs={{0,1},{1,0},{2,3},{3,2},{4,5},{5,4},{6,7},{7,6}} | collective-permute-start | bytes 25362440 | tf_op jit(solution)/shard_map/ppermute | solution.py:423
  680.8 309.5 %all-gather.46.cloned.1.call-start = ((), (), s32[]{:S(2)}) async-start(), calls=%async_computation.10 | async-start | bytes 10567680 | tf_op jit(solution)/shard_map/all_gather | solution.py:421
  811.2 24.9 %collective-permute-start.8 = (bf16[4,2064,512]{2,1,0:T(8,128)(2,1)}, bf16[4,2064,512]{2,1,0:T(8,128)(2,1)}, u32[]{:S(2)}, u32[]{:S(2)}) collective-permute-start(bf16[4,2064,512]{2,1,0:T(8,128)(2,1)} %bitcast.31), channel_id=1, source_target_pairs={{0,1},{1,0},{2,3},{3,2},{4,5},{5,4},{6,7},{7,6}} | collective-permute-start | bytes 25362440 | tf_op jit(solution)/shard_map/ppermute | solution.py:423
  836.1 309.0 %all-gather.48.cloned.1.call-start = ((), (), s32[]{:S(2)}) async-start(), calls=%async_computation.11 | async-start | bytes 10567680 | tf_op jit(solution)/shard_map/all_gather | solution.py:421
  965.7 25.0 %collective-permute-start.9 = (bf16[4,2064,512]{2,1,0:T(8,128)(2,1)}, bf16[4,2064,512]{2,1,0:T(8,128)(2,1)}, u32[]{:S(2)}, u32[]{:S(2)}) collective-permute-start(bf16[4,2064,512]{2,1,0:T(8,128)(2,1)} %bitcast.28), channel_id=1, source_target_pairs={{0,1},{1,0},{2,3},{3,2},{4,5},{5,4},{6,7},{7,6}} | collective-permute-start | bytes 25362440 | tf_op jit(solution)/shard_map/ppermute | solution.py:423
  990.4 237.2 %all-gather.50.cloned.1.call-start = ((), (), s32[]{:S(2)}) async-start(), calls=%async_computation.12 | async-start | bytes 10567680 | tf_op jit(solution)/shard_map/all_gather | solution.py:421
  1145.1 13.2 %collective-permute-start.11 = (bf16[4,2064,512]{2,1,0:T(8,128)(2,1)}, bf16[4,2064,512]{2,1,0:T(8,128)(2,1)}, u32[]{:S(2)}, u32[]{:S(2)}) collective-permute-start(bf16[4,2064,512]{2,1,0:T(8,128)(2,1)} %bitcast.25), channel_id=1, source_target_pairs={{0,1},{1,0},{2,3},{3,2},{4,5},{5,4},{6,7},{7,6}} | collective-permute-start | bytes 25362440 | tf_op jit(solution)/shard_map/ppermute | solution.py:423
  1145.3 32.1 %collective-permute-start.10 = (bf16[4,2064,512]{2,1,0:T(8,128)(2,1)}, bf16[4,2064,512]{2,1,0:T(8,128)(2,1)}, u32[]{:S(2)}, u32[]{:S(2)}) collective-permute-start(bf16[4,2064,512]{2,1,0:T(8,128)(2,1)} %bitcast.34), channel_id=1, source_target_pairs={{0,1},{1,0},{2,3},{3,2},{4,5},{5,4},{6,7},{7,6}} | collective-permute-start | bytes 25362440 | tf_op jit(solution)/shard_map/ppermute | solution.py:423
  1227.6 13.2 %collective-permute-start.12 = (bf16[4,2064,512]{2,1,0:T(8,128)(2,1)}, bf16[4,2064,512]{2,1,0:T(8,128)(2,1)}, u32[]{:S(2)}, u32[]{:S(2)}) collective-permute-start(bf16[4,2064,512]{2,1,0:T(8,128)(2,1)} %bitcast.37), channel_id=1, source_target_pairs={{0,1},{1,0},{2,3},{3,2},{4,5},{5,4},{6,7},{7,6}} | collective-permute-start | bytes 25362440 | tf_op jit(solution)/shard_map/ppermute | solution.py:427
  (2 other events, 20.2 us)
Sparse Core Ops, SparseCore 0:
  10.3 49.5 all-gather.25
  62.3 46.6 all-gather.27
  110.8 46.6 all-gather.31
  159.7 46.6 all-gather.33
  208.0 46.6 all-gather.29
  256.3 88.3 all-gather.35
  346.5 46.6 all-gather.37
  430.9 124.0 all-gather.39
  556.8 123.9 all-gather.41
  682.4 127.5 all-gather.43
  836.2 127.6 all-gather.45
  990.5 128.1 all-gather.47
  1145.2 82.4 all-gather.49

commit v3 on v1

--- a/solution.py
+++ b/solution.py
@@ -271,7 +271,8 @@
     )(e_seq, gates, c_seq, c_seq, w_stack)
 
 
-def weight_kernel(n, rows, hidden, land_ref, u_own, u_other, h_own, h_other, out_ref, acc, db_acc, dz_t, dz_shift):
+def weight_kernel(n, rows, hidden, land_ref, u_own, u_other, h_own, h_other, *refs):
+    *out_refs, acc, db_acc, dz_t = refs
     s = pl.program_id(0)
     share = land_ref.shape[-1]
 
@@ -282,16 +283,16 @@
 
     db_acc[...] += land_ref[0, pl.ds(n, EXTRA), :].astype(jnp.float32)
     dz_t[...] = land_ref[0, pl.ds(0, n), :].T
-    dz_shift[...] = jnp.concatenate([land_ref[0, pl.ds(rows, n - rows), :], jnp.zeros((rows, share), jnp.bfloat16)], axis=0).T
     part = 256
 
     def add(u_ref, h_ref):
         @pl.loop(0, hidden // part)
         def _(p):
-            for base, lhs, rhs in ((0, dz_t, u_ref), (hidden, dz_shift, h_ref)):
-                cols = pl.ds(pl.multiple_of(base + p * part, part), part)
-                rc = pl.ds(pl.multiple_of(p * part, part), part)
-                dw = jnp.dot(lhs[...], rhs[0, :, rc], preferred_element_type=jnp.float32)
+            rc = pl.ds(pl.multiple_of(p * part, part), part)
+            hc = pl.ds(pl.multiple_of(hidden + p * part, part), part)
+            h_prev = jnp.concatenate([jnp.zeros((rows, part), jnp.bfloat16), h_ref[0, pl.ds(0, n - rows), rc]], axis=0)
+            for cols, rhs in ((rc, u_ref[0, :, rc]), (hc, h_prev)):
+                dw = jnp.dot(dz_t[...], rhs, preferred_element_type=jnp.float32)
                 acc[:, cols] += dw.astype(jnp.bfloat16).astype(jnp.float32)
 
     @pl.when(s < CHIPS)
@@ -304,30 +305,32 @@
 
     @pl.when(s == PEERS - 1)
     def _():
-        @pl.loop(0, 2 * hidden // part)
-        def _(p):
-            cols = pl.ds(pl.multiple_of(p * part, part), part)
-            out_ref[cols, :] = acc[:, cols].T.astype(jnp.bfloat16)
-
-        out_ref[pl.ds(2 * hidden, EXTRA), :] = db_acc[...].astype(jnp.bfloat16)
-
-
-def weight_gradient(land, u_all, h_all, rows):
+        height = 2 * hidden // len(out_refs)
+        for half, out_ref in enumerate(out_refs):
+            @pl.loop(0, height // part)
+            def _(p):
+                cols = pl.ds(pl.multiple_of(half * height + p * part, part), part)
+                out_ref[pl.ds(pl.multiple_of(p * part, part), part), :] = acc[:, cols].T.astype(jnp.bfloat16)
+
+        out_refs[-1][pl.ds(height, EXTRA), :] = db_acc[...].astype(jnp.bfloat16)
+
+
+def weight_gradient(land, u_all, h_all, rows, pieces):
     _, height, share = land.shape
     _, n, hidden = u_all[0].shape
+    heights = [2 * hidden // pieces] * (pieces - 1) + [2 * hidden // pieces + EXTRA]
     own = pl.BlockSpec((1, n, hidden), lambda s: (jnp.minimum(s, CHIPS - 1), 0, 0))
     other = pl.BlockSpec((1, n, hidden), lambda s: (jnp.maximum(s - CHIPS, 0), 0, 0))
     return pl.pallas_call(
         functools.partial(weight_kernel, n, rows, hidden),
         grid=(PEERS,),
         in_specs=[pl.BlockSpec((1, height, share), lambda s: (s, 0, 0)), own, other, own, other],
-        out_specs=pl.BlockSpec((2 * hidden + EXTRA, share), lambda s: (0, 0)),
-        out_shape=jax.ShapeDtypeStruct((2 * hidden + EXTRA, share), jnp.bfloat16),
+        out_specs=[pl.BlockSpec((h, share), lambda s: (0, 0)) for h in heights],
+        out_shape=[jax.ShapeDtypeStruct((h, share), jnp.bfloat16) for h in heights],
         scratch_shapes=[
             pltpu.VMEM((share, 2 * hidden), jnp.float32),
             pltpu.VMEM((EXTRA, share), jnp.float32),
             pltpu.VMEM((share, n), jnp.bfloat16),
-            pltpu.VMEM((share, n), jnp.bfloat16),
         ],
         compiler_params=pltpu.CompilerParams(vmem_limit_bytes=VMEM_LIMIT),
         cost_estimate=pl.CostEstimate(flops=2 * PEERS * n * share * 2 * hidden * 4, bytes_accessed=4 * PEERS * n * hidden, transcendentals=0),
@@ -335,45 +338,49 @@
     )(land, *u_all, *h_all)
 
 
-def cast_kernel(core_ref, own_ref, other_ref, own_db, other_db, *refs):
-    out_ref, db_ref = refs[-2:]
+def cast_kernel(with_db, core_ref, own_ref, other_ref, *refs):
     core = core_ref[0]
     share = own_ref.shape[-1]
+    out_ref = refs[-2] if with_db else refs[-1]
     for chip in range(CHIPS):
-        for which, src, src_db in ((core, own_ref, own_db), (1 - core, other_ref, other_db)):
+        for i, (which, src) in enumerate(((core, own_ref), (1 - core, other_ref))):
             cols = pl.ds(pl.multiple_of((chip * 2 + which) * share, share), share)
             out_ref[0, :, cols] = src[chip].astype(jnp.float32)
-            db_ref[0, :, cols] = src_db[chip, pl.ds(0, 8), :][0:1].astype(jnp.float32)
-
-
-def cast_into(bufs, core, parts, layer, layers):
-    own, other = parts
-    _, height, share = own.shape
-    height -= EXTRA
+            if with_db:
+                refs[-1][0, :, cols] = refs[i][chip, pl.ds(0, 8), :][0:1].astype(jnp.float32)
+
+
+def cast_into(bufs, core, parts, layer, layers, first, hidden):
+    _, height, share = parts[0].shape
+    with_db = height % 128 != 0
+    height -= EXTRA if with_db else 0
     tile = 128
     width = PEERS * share
     big = pl.BlockSpec((CHIPS, tile, share), lambda i: (0, i, 0))
     small = pl.BlockSpec((CHIPS, EXTRA, share), lambda i: (0, height // EXTRA, 0))
-    return pl.pallas_call(
-        cast_kernel,
+    outs = 2 if with_db else 1
+    bufs = list(bufs)
+    operands = [core, *parts] + (list(parts) if with_db else [])
+    dw_db = pl.pallas_call(
+        functools.partial(cast_kernel, with_db),
         grid=(height // tile,),
-        in_specs=[pl.BlockSpec(memory_space=pltpu.SMEM), big, big, small, small] + [pl.BlockSpec(memory_space=pl.ANY)] * len(bufs),
-        out_specs=[pl.BlockSpec((1, tile, width), lambda i: (layer, i, 0)), pl.BlockSpec((1, 1, width), lambda i: (layer, 0, 0))],
-        out_shape=[jax.ShapeDtypeStruct((layers, height, width), jnp.float32), jax.ShapeDtypeStruct((layers, 1, width), jnp.float32)],
-        input_output_aliases={5: 0, 6: 1} if bufs else {},
+        in_specs=[pl.BlockSpec(memory_space=pltpu.SMEM), big, big] + [small] * (len(operands) - 3) + [pl.BlockSpec(memory_space=pl.ANY)] * (outs if bufs else 0),
+        out_specs=[pl.BlockSpec((1, tile, width), lambda i: (layer, first // tile + i, 0)), pl.BlockSpec((1, 1, width), lambda i: (layer, 0, 0))][:outs],
+        out_shape=[jax.ShapeDtypeStruct((layers, 2 * hidden, width), jnp.float32), jax.ShapeDtypeStruct((layers, 1, width), jnp.float32)][:outs],
+        input_output_aliases={len(operands) + k: k for k in range(outs)} if bufs else {},
         compiler_params=pltpu.CompilerParams(vmem_limit_bytes=VMEM_LIMIT),
         cost_estimate=pl.CostEstimate(flops=height * width * 100, bytes_accessed=6 * height * width, transcendentals=0),
         name="cast_gradient",
-    )(core, own, other, own, other, *bufs)
+    )(*operands, *bufs[:outs])
+    return list(dw_db) + bufs[outs:]
 
 
 def solution(mesh):
     batch_axes = ('replica', 'data')
     swap = [(0, 1), (1, 0)]
 
-    def gather(part):
-        own = lax.all_gather(part, 'replica')
-        return own, lax.ppermute(own, 'data', swap)
+    def tie(*values):
+        return lax.optimization_barrier(values)
 
     def local_grads(x_loc, dy_loc, w_stack, b_stack):
         layers = w_stack.shape[0]
@@ -382,26 +389,49 @@
         core = lax.axis_index('data').astype(jnp.int32).reshape(1)
         u = jnp.swapaxes(x_loc, 0, 1).reshape(n, hidden)
         b_rows = b_stack[:, None, :]
-        gathered = [gather(u)]
+        own = []
+        other = []
         saved = []
         for layer in range(layers):
+            own.append(lax.all_gather(u, 'replica'))
+            if layer >= 2:
+                u, own[layer - 2] = tie(u, own[layer - 2])
+                other.append(lax.ppermute(own[layer - 2], 'data', swap))
+            if layer >= 3:
+                u, other[layer - 3] = tie(u, other[layer - 3])
             gates, c_seq, u = forward(layer, u, w_stack, b_rows, steps)
             saved.append((gates, c_seq))
-            gathered.append(gather(u))
+        own.append(lax.all_gather(u, 'replica'))
         e_seq = jnp.swapaxes(dy_loc, 0, 1).reshape(n, hidden)
-        bufs = ()
+        e_seq, own[layers - 2], other[layers - 3] = tie(e_seq, own[layers - 2], other[layers - 3])
+        other.append(lax.ppermute(own[layers - 2], 'data', swap))
+        bufs = []
+        shard = None
         pending = None
         for layer in reversed(range(layers)):
             land, e_seq = backward(layer, e_seq, *saved[layer], w_stack, steps)
-            part = weight_gradient(land, gathered[layer], gathered[layer + 1], rows)
-            part, e_seq = lax.optimization_barrier((part, e_seq))
+            if layer == layers - 1:
+                land, own[layers - 1], own[layers] = tie(land, own[layers - 1], own[layers])
+                other.append(lax.ppermute(own[layers - 1], 'data', swap))
+                other.append(lax.ppermute(own[layers], 'data', swap))
             if pending is not None:
-                part, pending = lax.optimization_barrier((part, pending))
-            parts = gather(part)
-            if pending is not None:
-                bufs = cast_into(bufs, core, pending, layer + 1, layers)
-            pending = parts
-        dw, db = cast_into(bufs, core, pending, 0, layers)
-        return dw, db.reshape(layers, 4 * hidden), jnp.swapaxes(e_seq.reshape(steps, rows, hidden), 0, 1)
+                done_own, done_other, e_seq = tie(*pending, e_seq)
+                bufs = cast_into(bufs, core, (done_own, done_other), layer + 2, layers, 0, hidden)
+            parts = weight_gradient(land, (own[layer], other[layer]), (own[layer + 1], other[layer + 1]), rows, 1 if layer else 2)
+            *parts, e_seq = tie(*parts, e_seq)
+            if shard is not None:
+                *parts, shard = tie(*parts, shard)
+                if bufs:
+                    parts[0], bufs[1] = tie(parts[0], bufs[1])
+                pending = (shard, lax.ppermute(shard, 'data', swap))
+            shard = lax.all_gather(parts[0], 'replica')
+        bufs = cast_into(bufs, core, pending, 1, layers, 0, hidden)
+        dx = jnp.swapaxes(e_seq.reshape(steps, rows, hidden), 0, 1)
+        top, bottom, dx, bufs[1] = tie(shard, parts[1], dx, bufs[1])
+        bottom = lax.all_gather(bottom, 'replica')
+        bufs = cast_into(bufs, core, (top, lax.ppermute(top, 'data', swap)), 0, layers, 0, hidden)
+        bottom, bufs[0] = tie(bottom, bufs[0])
+        dw, db = cast_into(bufs, core, (bottom, lax.ppermute(bottom, 'data', swap)), 0, layers, hidden, hidden)
+        return dw, db.reshape(layers, 4 * hidden), dx
 
     return jax.shard_map(local_grads, mesh=mesh, in_specs=(P(batch_axes), P(batch_axes), P(), P()), out_specs=(P(), P(), P(batch_axes)), check_vma=False)

time: 1730 us -> 1220 us (0.71)
  waiting for transfers between devices: 835 us -> 187 us
  Pallas kernels: 863 us -> 988 us
    all_gather x13 -> x14, waiting for transfers between devices: 831 us -> 160 us  [the longest x7 81.4 us: local_grads(): own.append(lax.all_gather(u, 'replica'))]
    pallas_call x6, Pallas kernels: 399 us -> 528 us  [backward(): pl.pallas_call(functools.partial(backward_kernel, layer, steps, rows, hid...]
    ppermute x13 -> x14, waiting for transfers between devices: 0.03 us -> 26.9 us  [the longest x1 7.2 us: local_grads(): lax.ppermute(bottom, 'data', swap)]
    pallas_call x6 -> x7, Pallas kernels: 115 us -> 116 us  [cast_into(): pl.pallas_call(functools.partial(cast_kernel, with_db), grid=(height // t...]
  transfers between devices with their start and end apart: 26 -> 28, of which waited for: 13 -> 12; matrix products, arithmetic and copies ran while one was open for 0% -> 1% of each run, Pallas kernels for 36% -> 79%
where the time goes in v3:
time: 1220 us; the launch traced here: 1210 us
  Pallas kernels  988 us (81%)
  waiting for transfers between devices  187 us (15%)
  between operations  14.5 us (1%)
  local copies, waits for them, and re-layouts  14.3 us (1%)
    pallas_call x6, Pallas kernels, backward(): pl.pallas_call(functools.partial(backward_kernel, layer, steps, rows, hid...  528 us
    pallas_call x6, Pallas kernels, forward(): pl.pallas_call(functools.partial(forward_kernel, layer, steps, n // steps...  203 us
    pallas_call x6, Pallas kernels, weight_gradient(): pl.pallas_call(functools.partial(weight_kernel, n, rows, hidden), grid=(P...  141 us
    pallas_call x7, Pallas kernels, cast_into(): pl.pallas_call(functools.partial(cast_kernel, with_db), grid=(height // t...  116 us
    all_gather x7, waiting for transfers between devices, local_grads(): own.append(lax.all_gather(u, 'replica'))  81.4 us
    all_gather x6, waiting for transfers between devices, local_grads(): shard = lax.all_gather(parts[0], 'replica')  47.2 us
    all_gather x1, waiting for transfers between devices, local_grads(): bottom = lax.all_gather(bottom, 'replica')  31.7 us
  transfers between devices with their start and end apart: 28, of which 12 were waited for; matrix products, arithmetic and copies ran while one was open for 1% of the time, Pallas kernels for 79%

profile of v3, /device:TPU:0, one launch (start us, length us, event | category | flops | bytes accessed | tf_op | source)
XLA Modules:
  0.0 1210.5 jit_solution(12405309829365863905)
XLA Ops:
  11.7 33.8 %lstm_forward.6 = (f32[512,4096]{1,0:T(8,128)}, f32[512,1024]{1,0:T(8,128)}, bf16[512,1024]{1,0:T(8,128)(2,1)}) custom-call(bf16[512,1024]{1,0:T(8,128)(2,1)} %bitcast.47, bf16[6,2048,4096]{2,1,0:T(8,128)(2,1)} %w_hbm.23, f32[6,1,4096]{2,1,0:T(1,128)} %broadcast_in_dim.3.b_ref), custom_call_target="tpu_custom_call" | custom-call | flops 34359738368 | bytes 16777216 | tf_op jit(solution)/shard_map/lstm_forward/pallas_call | solution.py:87
  45.5 33.8 %lstm_forward.7 = (f32[512,4096]{1,0:T(8,128)}, f32[512,1024]{1,0:T(8,128)}, bf16[512,1024]{1,0:T(8,128)(2,1)}) custom-call(bf16[512,1024]{1,0:T(8,128)(2,1)} %get-tuple-element.117.u_ref, bf16[6,2048,4096]{2,1,0:T(8,128)(2,1)} %w_hbm.23, f32[6,1,4096]{2,1,0:T(1,128)} %broadcast_in_dim.3.b_ref), custom_call_target="tpu_custom_call" | custom-call | flops 34359738368 | bytes 16777216 | tf_op jit(solution)/shard_map/lstm_forward/pallas_call | solution.py:87
  80.5 33.8 %lstm_forward.8 = (f32[512,4096]{1,0:T(8,128)}, f32[512,1024]{1,0:T(8,128)}, bf16[512,1024]{1,0:T(8,128)(2,1)}) custom-call(bf16[512,1024]{1,0:T(8,128)(2,1)} %get-tuple-element.119.u_ref, bf16[6,2048,4096]{2,1,0:T(8,128)(2,1)} %w_hbm.23, f32[6,1,4096]{2,1,0:T(1,128)} %broadcast_in_dim.3.b_ref), custom_call_target="tpu_custom_call" | custom-call | flops 34359738368 | bytes 16777216 | tf_op jit(solution)/shard_map/lstm_forward/pallas_call | solution.py:87
  114.4 33.8 %lstm_forward.9 = (f32[512,4096]{1,0:T(8,128)}, f32[512,1024]{1,0:T(8,128)}, bf16[512,1024]{1,0:T(8,128)(2,1)}) custom-call(bf16[512,1024]{1,0:T(8,128)(2,1)} %get-tuple-element.123.u_ref, bf16[6,2048,4096]{2,1,0:T(8,128)(2,1)} %w_hbm.23, f32[6,1,4096]{2,1,0:T(1,128)} %broadcast_in_dim.3.b_ref), custom_call_target="tpu_custom_call" | custom-call | flops 34359738368 | bytes 16777216 | tf_op jit(solution)/shard_map/lstm_forward/pallas_call | solution.py:87
  157.6 33.8 %lstm_forward.10 = (f32[512,4096]{1,0:T(8,128)}, f32[512,1024]{1,0:T(8,128)}, bf16[512,1024]{1,0:T(8,128)(2,1)}) custom-call(bf16[512,1024]{1,0:T(8,128)(2,1)} %get-tuple-element.127.u_ref, bf16[6,2048,4096]{2,1,0:T(8,128)(2,1)} %w_hbm.23, f32[6,1,4096]{2,1,0:T(1,128)} %broadcast_in_dim.3.b_ref), custom_call_target="tpu_custom_call" | custom-call | flops 34359738368 | bytes 16777216 | tf_op jit(solution)/shard_map/lstm_forward/pallas_call | solution.py:87
  206.5 33.8 %lstm_forward.11 = (f32[512,4096]{1,0:T(8,128)}, f32[512,1024]{1,0:T(8,128)}, bf16[512,1024]{1,0:T(8,128)(2,1)}) custom-call(bf16[512,1024]{1,0:T(8,128)(2,1)} %get-tuple-element.133.u_ref, bf16[6,2048,4096]{2,1,0:T(8,128)(2,1)} %w_hbm.23, f32[6,1,4096]{2,1,0:T(1,128)} %broadcast_in_dim.3.b_ref), custom_call_target="tpu_custom_call" | custom-call | flops 34359738368 | bytes 16777216 | tf_op jit(solution)/shard_map/lstm_forward/pallas_call | solution.py:87
  254.8 90.9 %lstm_backward.6 = (bf16[8,528,512]{2,1,0:T(8,128)(2,1)}, f32[512,1024]{1,0:T(8,128)}) custom-call(f32[512,1024]{1,0:T(8,128)} %bitcast.51, f32[512,4096]{1,0:T(8,128)} %get-tuple-element.134.gates_ref, f32[512,1024]{1,0:T(8,128)} %get-tuple-element.135.c_ref.cp_ref, f32[512,1024]{1,0:T(8,128)} %get-tuple-element.135.c_ref.cp_ref, bf16[6,2048,4096]{2,1,0:T(8,128)(2,1)} %w_hbm.23), custom_call_target="tpu_custom_call" | custom-call | flops 34359738368 | bytes 16777216 | tf_op jit(solution)/shard_map/lstm_backward/pallas_call | solution.py:241
  345.7 47.5 %all-gather.40.cloned.1.call-done = bf16[2048,1024]{1,0:T(8,128)(2,1)} async-done(((bf16[512,1024]{1,0:T(8,128)(2,1)}), bf16[2048,1024]{1,0:T(8,128)(2,1)}) %all-gather.40.cloned.1.call-update) | async-done | bytes 4194320 | tf_op jit(solution)/shard_map/all_gather | solution.py:404
  406.4 23.5 %weight_gradient.6 = bf16[2064,512]{1,0:T(8,128)(2,1)} custom-call(bf16[8,528,512]{2,1,0:T(8,128)(2,1)} %get-tuple-element.138.land_ref, bf16[4,512,1024]{2,1,0:T(8,128)(2,1)} %bitcast.67, bf16[4,512,1024]{2,1,0:T(8,128)(2,1)} %collective-permute-done.4.u_other.h_other, bf16[4,512,1024]{2,1,0:T(8,128)(2,1)} %bitcast.70, ...), custom_call_target="tpu_custom_call" | custom-call | flops 34359738368 | bytes 16777216 | tf_op jit(solution)/shard_map/weight_gradient/pallas_call | solution.py:324
  430.3 88.4 %lstm_backward.7 = (bf16[8,528,512]{2,1,0:T(8,128)(2,1)}, f32[512,1024]{1,0:T(8,128)}) custom-call(f32[512,1024]{1,0:T(8,128)} %get-tuple-element.142.e_ref, f32[512,4096]{1,0:T(8,128)} %get-tuple-element.143.gates_ref, f32[512,1024]{1,0:T(8,128)} %get-tuple-element.144.c_ref.cp_ref, f32[512,1024]{1,0:T(8,128)} %get-tuple-element.144.c_ref.cp_ref, ...), custom_call_target="tpu_custom_call" | custom-call | flops 34359738368 | bytes 16777216 | tf_op jit(solution)/shard_map/lstm_backward/pallas_call | solution.py:241
  518.8 23.6 %weight_gradient.7 = bf16[2064,512]{1,0:T(8,128)(2,1)} custom-call(bf16[8,528,512]{2,1,0:T(8,128)(2,1)} %get-tuple-element.145.land_ref, bf16[4,512,1024]{2,1,0:T(8,128)(2,1)} %bitcast.64, bf16[4,512,1024]{2,1,0:T(8,128)(2,1)} %collective-permute-done.6.u_other.h_other, bf16[4,512,1024]{2,1,0:T(8,128)(2,1)} %bitcast.68, ...), custom_call_target="tpu_custom_call" | custom-call | flops 34359738368 | bytes 16777216 | tf_op jit(solution)/shard_map/weight_gradient/pallas_call | solution.py:324
  554.3 84.5 %lstm_backward.8 = (bf16[8,528,512]{2,1,0:T(8,128)(2,1)}, f32[512,1024]{1,0:T(8,128)}) custom-call(f32[512,1024]{1,0:T(8,128)} %get-tuple-element.148.e_ref, f32[512,4096]{1,0:T(8,128)} %get-tuple-element.149.gates_ref, f32[512,1024]{1,0:T(8,128)} %get-tuple-element.150.c_ref.cp_ref, f32[512,1024]{1,0:T(8,128)} %get-tuple-element.150.c_ref.cp_ref, ...), custom_call_target="tpu_custom_call" | custom-call | flops 34359738368 | bytes 16777216 | tf_op jit(solution)/shard_map/lstm_backward/pallas_call | solution.py:241
  638.8 23.6 %weight_gradient.8 = bf16[2064,512]{1,0:T(8,128)(2,1)} custom-call(bf16[8,528,512]{2,1,0:T(8,128)(2,1)} %get-tuple-element.151.land_ref, bf16[4,512,1024]{2,1,0:T(8,128)(2,1)} %bitcast.61, bf16[4,512,1024]{2,1,0:T(8,128)(2,1)} %collective-permute-done.2.u_other.h_other, bf16[4,512,1024]{2,1,0:T(8,128)(2,1)} %bitcast.65, ...), custom_call_target="tpu_custom_call" | custom-call | flops 34359738368 | bytes 16777216 | tf_op jit(solution)/shard_map/weight_gradient/pallas_call | solution.py:324
  662.4 19.1 %cast_gradient.7 = (f32[6,2048,4096]{2,1,0:T(8,128)}, f32[6,1,4096]{2,1,0:T(1,128)}) custom-call(s32[1]{0:T(128)} %bitcast.core_ref, bf16[4,2064,512]{2,1,0:T(8,128)(2,1)} %bitcast.39, bf16[4,2064,512]{2,1,0:T(8,128)(2,1)} %collective-permute-done.7.other_ref.refs_1_, bf16[4,2064,512]{2,1,0:T(8,128)(2,1)} %bitcast.40, ...), custom_call_target="tpu_custom_call" | custom-call | flops 838860800 | bytes 50331648 | tf_op jit(solution)/shard_map/cast_gradient/pallas_call | solution.py:364
  682.2 88.2 %lstm_backward.9 = (bf16[8,528,512]{2,1,0:T(8,128)(2,1)}, f32[512,1024]{1,0:T(8,128)}) custom-call(f32[512,1024]{1,0:T(8,128)} %get-tuple-element.158.e_ref, f32[512,4096]{1,0:T(8,128)} %get-tuple-element.159.gates_ref, f32[512,1024]{1,0:T(8,128)} %get-tuple-element.160.c_ref.cp_ref, f32[512,1024]{1,0:T(8,128)} %get-tuple-element.160.c_ref.cp_ref, ...), custom_call_target="tpu_custom_call" | custom-call | flops 34359738368 | bytes 16777216 | tf_op jit(solution)/shard_map/lstm_backward/pallas_call | solution.py:241
  770.4 23.6 %weight_gradient.9 = bf16[2064,512]{1,0:T(8,128)(2,1)} custom-call(bf16[8,528,512]{2,1,0:T(8,128)(2,1)} %get-tuple-element.161.land_ref, bf16[4,512,1024]{2,1,0:T(8,128)(2,1)} %bitcast.58, bf16[4,512,1024]{2,1,0:T(8,128)(2,1)} %collective-permute-done.3.u_other.h_other, bf16[4,512,1024]{2,1,0:T(8,128)(2,1)} %bitcast.62, ...), custom_call_target="tpu_custom_call" | custom-call | flops 34359738368 | bytes 16777216 | tf_op jit(solution)/shard_map/weight_gradient/pallas_call | solution.py:324
  794.0 19.1 %cast_gradient.8 = (f32[6,2048,4096]{2,1,0:T(8,128)}, f32[6,1,4096]{2,1,0:T(1,128)}) custom-call(s32[1]{0:T(128)} %bitcast.core_ref, bf16[4,2064,512]{2,1,0:T(8,128)(2,1)} %bitcast.30, bf16[4,2064,512]{2,1,0:T(8,128)(2,1)} %collective-permute-done.8.other_ref.refs_1_, bf16[4,2064,512]{2,1,0:T(8,128)(2,1)} %bitcast.31, ...), custom_call_target="tpu_custom_call", output_to_operand_aliasing={{0}: (5, {}), {1}: (6, {})} | custom-call | flops 838860800 | bytes 50331648 | tf_op jit(solution)/shard_map/cast_gradient/pallas_call | solution.py:364
  813.9 88.1 %lstm_backward.10 = (bf16[8,528,512]{2,1,0:T(8,128)(2,1)}, f32[512,1024]{1,0:T(8,128)}) custom-call(f32[512,1024]{1,0:T(8,128)} %get-tuple-element.168.e_ref, f32[512,4096]{1,0:T(8,128)} %get-tuple-element.169.gates_ref, f32[512,1024]{1,0:T(8,128)} %get-tuple-element.170.c_ref.cp_ref, f32[512,1024]{1,0:T(8,128)} %get-tuple-element.170.c_ref.cp_ref, ...), custom_call_target="tpu_custom_call" | custom-call | flops 34359738368 | bytes 16777216 | tf_op jit(solution)/shard_map/lstm_backward/pallas_call | solution.py:241
  902.0 23.6 %weight_gradient.10 = bf16[2064,512]{1,0:T(8,128)(2,1)} custom-call(bf16[8,528,512]{2,1,0:T(8,128)(2,1)} %get-tuple-element.171.land_ref, bf16[4,512,1024]{2,1,0:T(8,128)(2,1)} %bitcast.55, bf16[4,512,1024]{2,1,0:T(8,128)(2,1)} %collective-permute-done.1.u_other.h_other, bf16[4,512,1024]{2,1,0:T(8,128)(2,1)} %bitcast.59, ...), custom_call_target="tpu_custom_call" | custom-call | flops 34359738368 | bytes 16777216 | tf_op jit(solution)/shard_map/weight_gradient/pallas_call | solution.py:324
  925.5 19.1 %cast_gradient.9 = (f32[6,2048,4096]{2,1,0:T(8,128)}, f32[6,1,4096]{2,1,0:T(1,128)}) custom-call(s32[1]{0:T(128)} %bitcast.core_ref, bf16[4,2064,512]{2,1,0:T(8,128)(2,1)} %bitcast.33, bf16[4,2064,512]{2,1,0:T(8,128)(2,1)} %collective-permute-done.9.other_ref.refs_1_, bf16[4,2064,512]{2,1,0:T(8,128)(2,1)} %bitcast.34, ...), custom_call_target="tpu_custom_call", output_to_operand_aliasing={{0}: (5, {}), {1}: (6, {})} | custom-call | flops 838860800 | bytes 50331648 | tf_op jit(solution)/shard_map/cast_gradient/pallas_call | solution.py:364
  945.7 88.1 %lstm_backward.11 = (bf16[8,528,512]{2,1,0:T(8,128)(2,1)}, f32[512,1024]{1,0:T(8,128)}) custom-call(f32[512,1024]{1,0:T(8,128)} %get-tuple-element.182.e_ref, f32[512,4096]{1,0:T(8,128)} %get-tuple-element.183.gates_ref, f32[512,1024]{1,0:T(8,128)} %get-tuple-element.184.c_ref.cp_ref, f32[512,1024]{1,0:T(8,128)} %get-tuple-element.184.c_ref.cp_ref, ...), custom_call_target="tpu_custom_call" | custom-call | flops 34359738368 | bytes 16777216 | tf_op jit(solution)/shard_map/lstm_backward/pallas_call | solution.py:241
  1033.8 23.7 %weight_gradient.11 = (bf16[1024,512]{1,0:T(8,128)(2,1)}, bf16[1040,512]{1,0:T(8,128)(2,1)}) custom-call(bf16[8,528,512]{2,1,0:T(8,128)(2,1)} %get-tuple-element.185.land_ref, bf16[4,512,1024]{2,1,0:T(8,128)(2,1)} %all-gather.28.cloned.1.call-done.u_own, bf16[4,512,1024]{2,1,0:T(8,128)(2,1)} %collective-permute-done.u_other, bf16[4,512,1024]{2,1,0:T(8,128)(2,1)} %bitcast.56, ...), custom_call_target="tpu_custom_call" | custom-call | flops 34359738368 | bytes 16777216 | tf_op jit(solution)/shard_map/weight_gradient/pallas_call | solution.py:324
  1111.8 23.6 %all-gather.52.cloned.1.call-done = bf16[4096,512]{1,0:T(8,128)(2,1)} async-done(((bf16[1024,512]{1,0:T(8,128)(2,1)}), bf16[4096,512]{1,0:T(8,128)(2,1)}) %all-gather.52.cloned.1.call-update) | async-done | bytes 4194320 | tf_op jit(solution)/shard_map/all_gather | solution.py:427
  1152.7 31.7 %all-gather.54.cloned.1.call-done = bf16[4160,512]{1,0:T(8,128)(2,1)} async-done(((bf16[1040,512]{1,0:T(8,128)(2,1)}), bf16[4160,512]{1,0:T(8,128)(2,1)}) %all-gather.54.cloned.1.call-update) | async-done | bytes 4259856 | tf_op jit(solution)/shard_map/all_gather | solution.py:431
  (76 shorter events, 163.6 us)
Async XLA Ops:
  7.2 72.5 %all-gather.28.cloned.1.call-start = ((), (), s32[]{:S(2)}) async-start(), calls=%async_computation | async-start | bytes 5242880 | tf_op jit(solution)/shard_map/all_gather | solution.py:396
  10.0 104.4 %all-gather.30.cloned.1.call-start = ((), (), s32[]{:S(2)}) async-start(), calls=%async_computation.1 | async-start | bytes 5242880 | tf_op jit(solution)/shard_map/all_gather | solution.py:396
  45.5 112.1 %all-gather.34.cloned.1.call-start = ((), (), s32[]{:S(2)}) async-start(), calls=%async_computation.3 | async-start | bytes 5242880 | tf_op jit(solution)/shard_map/all_gather | solution.py:396
  79.4 127.1 %all-gather.36.cloned.1.call-start = ((), (), s32[]{:S(2)}) async-start(), calls=%async_computation.4 | async-start | bytes 5242880 | tf_op jit(solution)/shard_map/all_gather | solution.py:396
  79.7 34.8 %collective-permute-start = (bf16[4,512,1024]{2,1,0:T(8,128)(2,1)}, bf16[4,512,1024]{2,1,0:T(8,128)(2,1)}, u32[]{:S(2)}, u32[]{:S(2)}) collective-permute-start(bf16[4,512,1024]{2,1,0:T(8,128)(2,1)} %all-gather.28.cloned.1.call-done.u_own), channel_id=1, source_target_pairs={{0,1},{1,0},{2,3},{3,2},{4,5},{5,4},{6,7},{7,6}} | collective-permute-start | bytes 12582920 | tf_op jit(solution)/shard_map/ppermute | solution.py:399
  114.3 140.4 %all-gather.32.cloned.1.call-start = ((), (), s32[]{:S(2)}) async-start(), calls=%async_computation.2 | async-start | bytes 5242880 | tf_op jit(solution)/shard_map/all_gather | solution.py:396
  114.4 43.2 %collective-permute-start.1 = (bf16[4,512,1024]{2,1,0:T(8,128)(2,1)}, bf16[4,512,1024]{2,1,0:T(8,128)(2,1)}, u32[]{:S(2)}, u32[]{:S(2)}) collective-permute-start(bf16[4,512,1024]{2,1,0:T(8,128)(2,1)} %bitcast.54), channel_id=1, source_target_pairs={{0,1},{1,0},{2,3},{3,2},{4,5},{5,4},{6,7},{7,6}} | collective-permute-start | bytes 12582920 | tf_op jit(solution)/shard_map/ppermute | solution.py:399
  148.3 197.5 %all-gather.38.cloned.1.call-start = ((), (), s32[]{:S(2)}) async-start(), calls=%async_computation.5 | async-start | bytes 5242880 | tf_op jit(solution)/shard_map/all_gather | solution.py:396
  157.6 48.9 %collective-permute-start.3 = (bf16[4,512,1024]{2,1,0:T(8,128)(2,1)}, bf16[4,512,1024]{2,1,0:T(8,128)(2,1)}, u32[]{:S(2)}, u32[]{:S(2)}) collective-permute-start(bf16[4,512,1024]{2,1,0:T(8,128)(2,1)} %bitcast.57), channel_id=1, source_target_pairs={{0,1},{1,0},{2,3},{3,2},{4,5},{5,4},{6,7},{7,6}} | collective-permute-start | bytes 12582920 | tf_op jit(solution)/shard_map/ppermute | solution.py:399
  191.4 201.8 %all-gather.40.cloned.1.call-start = ((), (), s32[]{:S(2)}) async-start(), calls=%async_computation.6 | async-start | bytes 5242880 | tf_op jit(solution)/shard_map/all_gather | solution.py:404
  206.5 48.3 %collective-permute-start.2 = (bf16[4,512,1024]{2,1,0:T(8,128)(2,1)}, bf16[4,512,1024]{2,1,0:T(8,128)(2,1)}, u32[]{:S(2)}, u32[]{:S(2)}) collective-permute-start(bf16[4,512,1024]{2,1,0:T(8,128)(2,1)} %bitcast.60), channel_id=1, source_target_pairs={{0,1},{1,0},{2,3},{3,2},{4,5},{5,4},{6,7},{7,6}} | collective-permute-start | bytes 12582920 | tf_op jit(solution)/shard_map/ppermute | solution.py:399
  240.3 313.8 %all-gather.42.cloned.1.call-start = ((), (), s32[]{:S(2)}) async-start(), calls=%async_computation.7 | async-start | bytes 10567680 | tf_op jit(solution)/shard_map/all_gather | solution.py:427
  429.9 251.6 %all-gather.44.cloned.1.call-start = ((), (), s32[]{:S(2)}) async-start(), calls=%async_computation.8 | async-start | bytes 10567680 | tf_op jit(solution)/shard_map/all_gather | solution.py:427
  430.1 88.6 %collective-permute-start.6 = (bf16[4,512,1024]{2,1,0:T(8,128)(2,1)}, bf16[4,512,1024]{2,1,0:T(8,128)(2,1)}, u32[]{:S(2)}, u32[]{:S(2)}) collective-permute-start(bf16[4,512,1024]{2,1,0:T(8,128)(2,1)} %bitcast.63), channel_id=1, source_target_pairs={{0,1},{1,0},{2,3},{3,2},{4,5},{5,4},{6,7},{7,6}} | collective-permute-start | bytes 12582920 | tf_op jit(solution)/shard_map/ppermute | solution.py:407
  554.2 258.9 %all-gather.46.cloned.1.call-start = ((), (), s32[]{:S(2)}) async-start(), calls=%async_computation.9 | async-start | bytes 10567680 | tf_op jit(solution)/shard_map/all_gather | solution.py:427
  554.2 108.2 %collective-permute-start.7 = (bf16[4,2064,512]{2,1,0:T(8,128)(2,1)}, bf16[4,2064,512]{2,1,0:T(8,128)(2,1)}, u32[]{:S(2)}, u32[]{:S(2)}) collective-permute-start(bf16[4,2064,512]{2,1,0:T(8,128)(2,1)} %bitcast.38), channel_id=1, source_target_pairs={{0,1},{1,0},{2,3},{3,2},{4,5},{5,4},{6,7},{7,6}} | collective-permute-start | bytes 25362440 | tf_op jit(solution)/shard_map/ppermute | solution.py:426
  681.5 263.2 %all-gather.48.cloned.1.call-start = ((), (), s32[]{:S(2)}) async-start(), calls=%async_computation.10 | async-start | bytes 10567680 | tf_op jit(solution)/shard_map/all_gather | solution.py:427
  681.8 112.2 %collective-permute-start.8 = (bf16[4,2064,512]{2,1,0:T(8,128)(2,1)}, bf16[4,2064,512]{2,1,0:T(8,128)(2,1)}, u32[]{:S(2)}, u32[]{:S(2)}) collective-permute-start(bf16[4,2064,512]{2,1,0:T(8,128)(2,1)} %bitcast.29), channel_id=1, source_target_pairs={{0,1},{1,0},{2,3},{3,2},{4,5},{5,4},{6,7},{7,6}} | collective-permute-start | bytes 25362440 | tf_op jit(solution)/shard_map/ppermute | solution.py:426
  813.1 256.2 %all-gather.50.cloned.1.call-start = ((), (), s32[]{:S(2)}) async-start(), calls=%async_computation.11 | async-start | bytes 10567680 | tf_op jit(solution)/shard_map/all_gather | solution.py:427
  813.2 112.4 %collective-permute-start.9 = (bf16[4,2064,512]{2,1,0:T(8,128)(2,1)}, bf16[4,2064,512]{2,1,0:T(8,128)(2,1)}, u32[]{:S(2)}, u32[]{:S(2)}) collective-permute-start(bf16[4,2064,512]{2,1,0:T(8,128)(2,1)} %bitcast.32), channel_id=1, source_target_pairs={{0,1},{1,0},{2,3},{3,2},{4,5},{5,4},{6,7},{7,6}} | collective-permute-start | bytes 25362440 | tf_op jit(solution)/shard_map/ppermute | solution.py:426
  944.7 190.7 %all-gather.52.cloned.1.call-start = ((), (), s32[]{:S(2)}) async-start(), calls=%async_computation.12 | async-start | bytes 5242880 | tf_op jit(solution)/shard_map/all_gather | solution.py:427
  945.0 112.5 %collective-permute-start.10 = (bf16[4,2064,512]{2,1,0:T(8,128)(2,1)}, bf16[4,2064,512]{2,1,0:T(8,128)(2,1)}, u32[]{:S(2)}, u32[]{:S(2)}) collective-permute-start(bf16[4,2064,512]{2,1,0:T(8,128)(2,1)} %bitcast.26), channel_id=1, source_target_pairs={{0,1},{1,0},{2,3},{3,2},{4,5},{5,4},{6,7},{7,6}} | collective-permute-start | bytes 25362440 | tf_op jit(solution)/shard_map/ppermute | solution.py:426
  1069.3 23.4 %collective-permute-start.11 = (bf16[4,2064,512]{2,1,0:T(8,128)(2,1)}, bf16[4,2064,512]{2,1,0:T(8,128)(2,1)}, u32[]{:S(2)}, u32[]{:S(2)}) collective-permute-start(bf16[4,2064,512]{2,1,0:T(8,128)(2,1)} %bitcast.35), channel_id=1, source_target_pairs={{0,1},{1,0},{2,3},{3,2},{4,5},{5,4},{6,7},{7,6}} | collective-permute-start | bytes 25362440 | tf_op jit(solution)/shard_map/ppermute | solution.py:426
  1088.5 95.9 %all-gather.54.cloned.1.call-start = ((), (), s32[]{:S(2)}) async-start(), calls=%async_computation.13 | async-start | bytes 5324800 | tf_op jit(solution)/shard_map/all_gather | solution.py:431
  (4 other events, 34.5 us)
Sparse Core Ops, SparseCore 0:
  10.3 49.5 all-gather.27
  62.3 46.6 all-gather.29
  110.8 46.7 all-gather.33
  159.8 46.6 all-gather.35
  208.1 46.6 all-gather.31
  256.4 88.2 all-gather.37
  346.5 46.7 all-gather.39
  430.0 124.0 all-gather.41
  555.9 123.8 all-gather.43
  681.6 124.1 all-gather.45
  813.2 124.4 all-gather.47
  944.8 124.4 all-gather.49
  1088.6 46.7 all-gather.51
  1137.0 47.3 all-gather.53

commit v4 on v3

--- a/solution.py
+++ b/solution.py
@@ -286,10 +286,9 @@
     part = 256
 
     def add(u_ref, h_ref):
-        @pl.loop(0, hidden // part)
-        def _(p):
-            rc = pl.ds(pl.multiple_of(p * part, part), part)
-            hc = pl.ds(pl.multiple_of(hidden + p * part, part), part)
+        for p in range(hidden // part):
+            rc = pl.ds(p * part, part)
+            hc = pl.ds(hidden + p * part, part)
             h_prev = jnp.concatenate([jnp.zeros((rows, part), jnp.bfloat16), h_ref[0, pl.ds(0, n - rows), rc]], axis=0)
             for cols, rhs in ((rc, u_ref[0, :, rc]), (hc, h_prev)):
                 dw = jnp.dot(dz_t[...], rhs, preferred_element_type=jnp.float32)
@@ -310,7 +309,7 @@
             @pl.loop(0, height // part)
             def _(p):
                 cols = pl.ds(pl.multiple_of(half * height + p * part, part), part)
-                out_ref[pl.ds(pl.multiple_of(p * part, part), part), :] = acc[:, cols].T.astype(jnp.bfloat16)
+                out_ref[pl.ds(pl.multiple_of(p * part, part), part), :] = acc[:, cols].astype(jnp.bfloat16).T
 
         out_refs[-1][pl.ds(height, EXTRA), :] = db_acc[...].astype(jnp.bfloat16)
 
@@ -394,24 +393,25 @@
         saved = []
         for layer in range(layers):
             own.append(lax.all_gather(u, 'replica'))
-            if layer >= 2:
-                u, own[layer - 2] = tie(u, own[layer - 2])
-                other.append(lax.ppermute(own[layer - 2], 'data', swap))
             if layer >= 3:
-                u, other[layer - 3] = tie(u, other[layer - 3])
+                u, own[layer - 3] = tie(u, own[layer - 3])
+                other.append(lax.ppermute(own[layer - 3], 'data', swap))
+            if layer >= 4:
+                u, other[layer - 4] = tie(u, other[layer - 4])
             gates, c_seq, u = forward(layer, u, w_stack, b_rows, steps)
             saved.append((gates, c_seq))
         own.append(lax.all_gather(u, 'replica'))
         e_seq = jnp.swapaxes(dy_loc, 0, 1).reshape(n, hidden)
-        e_seq, own[layers - 2], other[layers - 3] = tie(e_seq, own[layers - 2], other[layers - 3])
-        other.append(lax.ppermute(own[layers - 2], 'data', swap))
+        e_seq, own[layers - 3], other[layers - 4] = tie(e_seq, own[layers - 3], other[layers - 4])
+        other.append(lax.ppermute(own[layers - 3], 'data', swap))
         bufs = []
         shard = None
         pending = None
         for layer in reversed(range(layers)):
             land, e_seq = backward(layer, e_seq, *saved[layer], w_stack, steps)
             if layer == layers - 1:
-                land, own[layers - 1], own[layers] = tie(land, own[layers - 1], own[layers])
+                land, own[layers - 2], own[layers - 1], own[layers] = tie(land, own[layers - 2], own[layers - 1], own[layers])
+                other.append(lax.ppermute(own[layers - 2], 'data', swap))
                 other.append(lax.ppermute(own[layers - 1], 'data', swap))
                 other.append(lax.ppermute(own[layers], 'data', swap))
             if pending is not None:
@@ -421,7 +421,7 @@
             *parts, e_seq = tie(*parts, e_seq)
             if shard is not None:
                 *parts, shard = tie(*parts, shard)
-                if bufs:
+                if bufs and layer:
                     parts[0], bufs[1] = tie(parts[0], bufs[1])
                 pending = (shard, lax.ppermute(shard, 'data', swap))
             shard = lax.all_gather(parts[0], 'replica')

time: 1220 us -> 1180 us (0.967)
  Pallas kernels: 988 us -> 950 us
    pallas_call x6, Pallas kernels: 141 us -> 106 us  [weight_gradient(): pl.pallas_call(functools.partial(weight_kernel, n, rows, hidden), grid=(P...]
where the time goes in v4:
time: 1180 us; the launch traced here: 1170 us
  Pallas kernels  950 us (81%)
  waiting for transfers between devices  184 us (16%)
  between operations  14.6 us (1%)
  local copies, waits for them, and re-layouts  14.3 us (1%)
    pallas_call x6, Pallas kernels, backward(): pl.pallas_call(functools.partial(backward_kernel, layer, steps, rows, hid...  525 us
    pallas_call x6, Pallas kernels, forward(): pl.pallas_call(functools.partial(forward_kernel, layer, steps, n // steps...  203 us
    pallas_call x7, Pallas kernels, cast_into(): pl.pallas_call(functools.partial(cast_kernel, with_db), grid=(height // t...  116 us
    pallas_call x6, Pallas kernels, weight_gradient(): pl.pallas_call(functools.partial(weight_kernel, n, rows, hidden), grid=(P...  106 us
    all_gather x7, waiting for transfers between devices, local_grads(): own.append(lax.all_gather(u, 'replica'))  79.6 us
    all_gather x6, waiting for transfers between devices, local_grads(): shard = lax.all_gather(parts[0], 'replica')  45.5 us
    all_gather x1, waiting for transfers between devices, local_grads(): bottom = lax.all_gather(bottom, 'replica')  31.7 us
  transfers between devices with their start and end apart: 28, of which 12 were waited for; matrix products, arithmetic and copies ran while one was open for 1% of the time, Pallas kernels for 79%

profile of v4, /device:TPU:0, one launch (start us, length us, event | category | flops | bytes accessed | tf_op | source)
XLA Modules:
  0.0 1169.4 jit_solution(131543493210302332)
XLA Ops:
  11.7 33.8 %lstm_forward.6 = (f32[512,4096]{1,0:T(8,128)}, f32[512,1024]{1,0:T(8,128)}, bf16[512,1024]{1,0:T(8,128)(2,1)}) custom-call(bf16[512,1024]{1,0:T(8,128)(2,1)} %bitcast.47, bf16[6,2048,4096]{2,1,0:T(8,128)(2,1)} %w_hbm.23, f32[6,1,4096]{2,1,0:T(1,128)} %broadcast_in_dim.3.b_ref), custom_call_target="tpu_custom_call" | custom-call | flops 34359738368 | bytes 16777216 | tf_op jit(solution)/shard_map/lstm_forward/pallas_call | solution.py:87
  45.6 33.8 %lstm_forward.7 = (f32[512,4096]{1,0:T(8,128)}, f32[512,1024]{1,0:T(8,128)}, bf16[512,1024]{1,0:T(8,128)(2,1)}) custom-call(bf16[512,1024]{1,0:T(8,128)(2,1)} %get-tuple-element.112.u_ref, bf16[6,2048,4096]{2,1,0:T(8,128)(2,1)} %w_hbm.23, f32[6,1,4096]{2,1,0:T(1,128)} %broadcast_in_dim.3.b_ref), custom_call_target="tpu_custom_call" | custom-call | flops 34359738368 | bytes 16777216 | tf_op jit(solution)/shard_map/lstm_forward/pallas_call | solution.py:87
  79.6 33.8 %lstm_forward.8 = (f32[512,4096]{1,0:T(8,128)}, f32[512,1024]{1,0:T(8,128)}, bf16[512,1024]{1,0:T(8,128)(2,1)}) custom-call(bf16[512,1024]{1,0:T(8,128)(2,1)} %get-tuple-element.113.u_ref, bf16[6,2048,4096]{2,1,0:T(8,128)(2,1)} %w_hbm.23, f32[6,1,4096]{2,1,0:T(1,128)} %broadcast_in_dim.3.b_ref), custom_call_target="tpu_custom_call" | custom-call | flops 34359738368 | bytes 16777216 | tf_op jit(solution)/shard_map/lstm_forward/pallas_call | solution.py:87
  114.4 33.8 %lstm_forward.9 = (f32[512,4096]{1,0:T(8,128)}, f32[512,1024]{1,0:T(8,128)}, bf16[512,1024]{1,0:T(8,128)(2,1)}) custom-call(bf16[512,1024]{1,0:T(8,128)(2,1)} %get-tuple-element.115.u_ref, bf16[6,2048,4096]{2,1,0:T(8,128)(2,1)} %w_hbm.23, f32[6,1,4096]{2,1,0:T(1,128)} %broadcast_in_dim.3.b_ref), custom_call_target="tpu_custom_call" | custom-call | flops 34359738368 | bytes 16777216 | tf_op jit(solution)/shard_map/lstm_forward/pallas_call | solution.py:87
  148.6 33.8 %lstm_forward.10 = (f32[512,4096]{1,0:T(8,128)}, f32[512,1024]{1,0:T(8,128)}, bf16[512,1024]{1,0:T(8,128)(2,1)}) custom-call(bf16[512,1024]{1,0:T(8,128)(2,1)} %get-tuple-element.119.u_ref, bf16[6,2048,4096]{2,1,0:T(8,128)(2,1)} %w_hbm.23, f32[6,1,4096]{2,1,0:T(1,128)} %broadcast_in_dim.3.b_ref), custom_call_target="tpu_custom_call" | custom-call | flops 34359738368 | bytes 16777216 | tf_op jit(solution)/shard_map/lstm_forward/pallas_call | solution.py:87
  183.1 33.8 %lstm_forward.11 = (f32[512,4096]{1,0:T(8,128)}, f32[512,1024]{1,0:T(8,128)}, bf16[512,1024]{1,0:T(8,128)(2,1)}) custom-call(bf16[512,1024]{1,0:T(8,128)(2,1)} %get-tuple-element.125.u_ref, bf16[6,2048,4096]{2,1,0:T(8,128)(2,1)} %w_hbm.23, f32[6,1,4096]{2,1,0:T(1,128)} %broadcast_in_dim.3.b_ref), custom_call_target="tpu_custom_call" | custom-call | flops 34359738368 | bytes 16777216 | tf_op jit(solution)/shard_map/lstm_forward/pallas_call | solution.py:87
  221.3 86.2 %lstm_backward.6 = (bf16[8,528,512]{2,1,0:T(8,128)(2,1)}, f32[512,1024]{1,0:T(8,128)}) custom-call(f32[512,1024]{1,0:T(8,128)} %bitcast.51, f32[512,4096]{1,0:T(8,128)} %get-tuple-element.126.gates_ref, f32[512,1024]{1,0:T(8,128)} %get-tuple-element.127.c_ref.cp_ref, f32[512,1024]{1,0:T(8,128)} %get-tuple-element.127.c_ref.cp_ref, bf16[6,2048,4096]{2,1,0:T(8,128)(2,1)} %w_hbm.23), custom_call_target="tpu_custom_call" | custom-call | flops 34359738368 | bytes 16777216 | tf_op jit(solution)/shard_map/lstm_backward/pallas_call | solution.py:241
  307.6 31.1 %all-gather.38.cloned.1.call-done = bf16[2048,1024]{1,0:T(8,128)(2,1)} async-done(((bf16[512,1024]{1,0:T(8,128)(2,1)}), bf16[2048,1024]{1,0:T(8,128)(2,1)}) %all-gather.38.cloned.1.call-update) | async-done | bytes 4194320 | tf_op jit(solution)/shard_map/all_gather | solution.py:395
  338.7 48.5 %all-gather.40.cloned.1.call-done = bf16[2048,1024]{1,0:T(8,128)(2,1)} async-done(((bf16[512,1024]{1,0:T(8,128)(2,1)}), bf16[2048,1024]{1,0:T(8,128)(2,1)}) %all-gather.40.cloned.1.call-update) | async-done | bytes 4194320 | tf_op jit(solution)/shard_map/all_gather | solution.py:403
  418.6 88.4 %lstm_backward.7 = (bf16[8,528,512]{2,1,0:T(8,128)(2,1)}, f32[512,1024]{1,0:T(8,128)}) custom-call(f32[512,1024]{1,0:T(8,128)} %get-tuple-element.134.e_ref, f32[512,4096]{1,0:T(8,128)} %get-tuple-element.135.gates_ref, f32[512,1024]{1,0:T(8,128)} %get-tuple-element.136.c_ref.cp_ref, f32[512,1024]{1,0:T(8,128)} %get-tuple-element.136.c_ref.cp_ref, ...), custom_call_target="tpu_custom_call" | custom-call | flops 34359738368 | bytes 16777216 | tf_op jit(solution)/shard_map/lstm_backward/pallas_call | solution.py:241
  542.9 85.2 %lstm_backward.8 = (bf16[8,528,512]{2,1,0:T(8,128)(2,1)}, f32[512,1024]{1,0:T(8,128)}) custom-call(f32[512,1024]{1,0:T(8,128)} %get-tuple-element.140.e_ref, f32[512,4096]{1,0:T(8,128)} %get-tuple-element.141.gates_ref, f32[512,1024]{1,0:T(8,128)} %get-tuple-element.142.c_ref.cp_ref, f32[512,1024]{1,0:T(8,128)} %get-tuple-element.142.c_ref.cp_ref, ...), custom_call_target="tpu_custom_call" | custom-call | flops 34359738368 | bytes 16777216 | tf_op jit(solution)/shard_map/lstm_backward/pallas_call | solution.py:241
  628.2 17.7 %weight_gradient.8 = bf16[2064,512]{1,0:T(8,128)(2,1)} custom-call(bf16[8,528,512]{2,1,0:T(8,128)(2,1)} %get-tuple-element.143.land_ref, bf16[4,512,1024]{2,1,0:T(8,128)(2,1)} %bitcast.61, bf16[4,512,1024]{2,1,0:T(8,128)(2,1)} %collective-permute-done.6.u_other.h_other, bf16[4,512,1024]{2,1,0:T(8,128)(2,1)} %bitcast.65, ...), custom_call_target="tpu_custom_call" | custom-call | flops 34359738368 | bytes 16777216 | tf_op jit(solution)/shard_map/weight_gradient/pallas_call | solution.py:323
  645.8 19.1 %cast_gradient.7 = (f32[6,2048,4096]{2,1,0:T(8,128)}, f32[6,1,4096]{2,1,0:T(1,128)}) custom-call(s32[1]{0:T(128)} %bitcast.core_ref, bf16[4,2064,512]{2,1,0:T(8,128)(2,1)} %bitcast.39, bf16[4,2064,512]{2,1,0:T(8,128)(2,1)} %collective-permute-done.7.other_ref.refs_1_, bf16[4,2064,512]{2,1,0:T(8,128)(2,1)} %bitcast.40, ...), custom_call_target="tpu_custom_call" | custom-call | flops 838860800 | bytes 50331648 | tf_op jit(solution)/shard_map/cast_gradient/pallas_call | solution.py:363
  668.4 88.8 %lstm_backward.9 = (bf16[8,528,512]{2,1,0:T(8,128)(2,1)}, f32[512,1024]{1,0:T(8,128)}) custom-call(f32[512,1024]{1,0:T(8,128)} %get-tuple-element.150.e_ref, f32[512,4096]{1,0:T(8,128)} %get-tuple-element.151.gates_ref, f32[512,1024]{1,0:T(8,128)} %get-tuple-element.152.c_ref.cp_ref, f32[512,1024]{1,0:T(8,128)} %get-tuple-element.152.c_ref.cp_ref, ...), custom_call_target="tpu_custom_call" | custom-call | flops 34359738368 | bytes 16777216 | tf_op jit(solution)/shard_map/lstm_backward/pallas_call | solution.py:241
  757.2 17.7 %weight_gradient.9 = bf16[2064,512]{1,0:T(8,128)(2,1)} custom-call(bf16[8,528,512]{2,1,0:T(8,128)(2,1)} %get-tuple-element.153.land_ref, bf16[4,512,1024]{2,1,0:T(8,128)(2,1)} %bitcast.58, bf16[4,512,1024]{2,1,0:T(8,128)(2,1)} %collective-permute-done.1.u_other.h_other, bf16[4,512,1024]{2,1,0:T(8,128)(2,1)} %bitcast.62, ...), custom_call_target="tpu_custom_call" | custom-call | flops 34359738368 | bytes 16777216 | tf_op jit(solution)/shard_map/weight_gradient/pallas_call | solution.py:323
  774.9 19.1 %cast_gradient.8 = (f32[6,2048,4096]{2,1,0:T(8,128)}, f32[6,1,4096]{2,1,0:T(1,128)}) custom-call(s32[1]{0:T(128)} %bitcast.core_ref, bf16[4,2064,512]{2,1,0:T(8,128)(2,1)} %bitcast.30, bf16[4,2064,512]{2,1,0:T(8,128)(2,1)} %collective-permute-done.8.other_ref.refs_1_, bf16[4,2064,512]{2,1,0:T(8,128)(2,1)} %bitcast.31, ...), custom_call_target="tpu_custom_call", output_to_operand_aliasing={{0}: (5, {}), {1}: (6, {})} | custom-call | flops 838860800 | bytes 50331648 | tf_op jit(solution)/shard_map/cast_gradient/pallas_call | solution.py:363
  794.8 88.3 %lstm_backward.10 = (bf16[8,528,512]{2,1,0:T(8,128)(2,1)}, f32[512,1024]{1,0:T(8,128)}) custom-call(f32[512,1024]{1,0:T(8,128)} %get-tuple-element.160.e_ref, f32[512,4096]{1,0:T(8,128)} %get-tuple-element.161.gates_ref, f32[512,1024]{1,0:T(8,128)} %get-tuple-element.162.c_ref.cp_ref, f32[512,1024]{1,0:T(8,128)} %get-tuple-element.162.c_ref.cp_ref, ...), custom_call_target="tpu_custom_call" | custom-call | flops 34359738368 | bytes 16777216 | tf_op jit(solution)/shard_map/lstm_backward/pallas_call | solution.py:241
  900.7 19.1 %cast_gradient.9 = (f32[6,2048,4096]{2,1,0:T(8,128)}, f32[6,1,4096]{2,1,0:T(1,128)}) custom-call(s32[1]{0:T(128)} %bitcast.core_ref, bf16[4,2064,512]{2,1,0:T(8,128)(2,1)} %bitcast.33, bf16[4,2064,512]{2,1,0:T(8,128)(2,1)} %collective-permute-done.9.other_ref.refs_1_, bf16[4,2064,512]{2,1,0:T(8,128)(2,1)} %bitcast.34, ...), custom_call_target="tpu_custom_call", output_to_operand_aliasing={{0}: (5, {}), {1}: (6, {})} | custom-call | flops 838860800 | bytes 50331648 | tf_op jit(solution)/shard_map/cast_gradient/pallas_call | solution.py:363
  920.7 88.5 %lstm_backward.11 = (bf16[8,528,512]{2,1,0:T(8,128)(2,1)}, f32[512,1024]{1,0:T(8,128)}) custom-call(f32[512,1024]{1,0:T(8,128)} %get-tuple-element.174.e_ref, f32[512,4096]{1,0:T(8,128)} %get-tuple-element.175.gates_ref, f32[512,1024]{1,0:T(8,128)} %get-tuple-element.176.c_ref.cp_ref, f32[512,1024]{1,0:T(8,128)} %get-tuple-element.176.c_ref.cp_ref, ...), custom_call_target="tpu_custom_call" | custom-call | flops 34359738368 | bytes 16777216 | tf_op jit(solution)/shard_map/lstm_backward/pallas_call | solution.py:241
  1009.2 17.7 %weight_gradient.11 = (bf16[1024,512]{1,0:T(8,128)(2,1)}, bf16[1040,512]{1,0:T(8,128)(2,1)}) custom-call(bf16[8,528,512]{2,1,0:T(8,128)(2,1)} %get-tuple-element.177.land_ref, bf16[4,512,1024]{2,1,0:T(8,128)(2,1)} %all-gather.28.cloned.1.call-done.u_own, bf16[4,512,1024]{2,1,0:T(8,128)(2,1)} %collective-permute-done.u_other, bf16[4,512,1024]{2,1,0:T(8,128)(2,1)} %bitcast.56, ...), custom_call_target="tpu_custom_call" | custom-call | flops 34359738368 | bytes 16777216 | tf_op jit(solution)/shard_map/weight_gradient/pallas_call | solution.py:323
  1026.9 18.8 %all-gather.50.cloned.1.call-done = bf16[8256,512]{1,0:T(8,128)(2,1)} async-done(((bf16[2064,512]{1,0:T(8,128)(2,1)}), bf16[8256,512]{1,0:T(8,128)(2,1)}) %all-gather.50.cloned.1.call-update) | async-done | bytes 8454160 | tf_op jit(solution)/shard_map/all_gather | solution.py:427
  1050.0 19.1 %cast_gradient.10 = (f32[6,2048,4096]{2,1,0:T(8,128)}, f32[6,1,4096]{2,1,0:T(1,128)}) custom-call(s32[1]{0:T(128)} %bitcast.core_ref, bf16[4,2064,512]{2,1,0:T(8,128)(2,1)} %bitcast.27, bf16[4,2064,512]{2,1,0:T(8,128)(2,1)} %collective-permute-done.10.other_ref.refs_1_, ...), custom_call_target="tpu_custom_call", output_to_operand_aliasing={{0}: (5, {}), {1}: (6, {})} | custom-call | flops 838860800 | bytes 50331648 | tf_op jit(solution)/shard_map/cast_gradient/pallas_call | solution.py:363
  1069.1 19.1 %cast_gradient.11 = (f32[6,2048,4096]{2,1,0:T(8,128)}, f32[6,1,4096]{2,1,0:T(1,128)}) custom-call(s32[1]{0:T(128)} %bitcast.core_ref, bf16[4,2064,512]{2,1,0:T(8,128)(2,1)} %bitcast.36, bf16[4,2064,512]{2,1,0:T(8,128)(2,1)} %collective-permute-done.11.other_ref.refs_1_, ...), custom_call_target="tpu_custom_call", output_to_operand_aliasing={{0}: (5, {}), {1}: (6, {})} | custom-call | flops 838860800 | bytes 50331648 | tf_op jit(solution)/shard_map/cast_gradient/pallas_call | solution.py:363
  1111.6 31.7 %all-gather.54.cloned.1.call-done = bf16[4160,512]{1,0:T(8,128)(2,1)} async-done(((bf16[1040,512]{1,0:T(8,128)(2,1)}), bf16[4160,512]{1,0:T(8,128)(2,1)}) %all-gather.54.cloned.1.call-update) | async-done | bytes 4259856 | tf_op jit(solution)/shard_map/all_gather | solution.py:431
  (76 shorter events, 147.9 us)
Async XLA Ops:
  7.2 106.4 %all-gather.28.cloned.1.call-start = ((), (), s32[]{:S(2)}) async-start(), calls=%async_computation | async-start | bytes 5242880 | tf_op jit(solution)/shard_map/all_gather | solution.py:395
  10.0 138.6 %all-gather.32.cloned.1.call-start = ((), (), s32[]{:S(2)}) async-start(), calls=%async_computation.2 | async-start | bytes 5242880 | tf_op jit(solution)/shard_map/all_gather | solution.py:395
  45.5 137.0 %all-gather.34.cloned.1.call-start = ((), (), s32[]{:S(2)}) async-start(), calls=%async_computation.3 | async-start | bytes 5242880 | tf_op jit(solution)/shard_map/all_gather | solution.py:395
  79.4 141.9 %all-gather.30.cloned.1.call-start = ((), (), s32[]{:S(2)}) async-start(), calls=%async_computation.1 | async-start | bytes 5242880 | tf_op jit(solution)/shard_map/all_gather | solution.py:395
  113.5 194.1 %all-gather.36.cloned.1.call-start = ((), (), s32[]{:S(2)}) async-start(), calls=%async_computation.4 | async-start | bytes 5242880 | tf_op jit(solution)/shard_map/all_gather | solution.py:395
  113.6 35.1 %collective-permute-start = (bf16[4,512,1024]{2,1,0:T(8,128)(2,1)}, bf16[4,512,1024]{2,1,0:T(8,128)(2,1)}, u32[]{:S(2)}, u32[]{:S(2)}) collective-permute-start(bf16[4,512,1024]{2,1,0:T(8,128)(2,1)} %all-gather.28.cloned.1.call-done.u_own), channel_id=1, source_target_pairs={{0,1},{1,0},{2,3},{3,2},{4,5},{5,4},{6,7},{7,6}} | collective-permute-start | bytes 12582920 | tf_op jit(solution)/shard_map/ppermute | solution.py:398
  148.3 190.4 %all-gather.38.cloned.1.call-start = ((), (), s32[]{:S(2)}) async-start(), calls=%async_computation.5 | async-start | bytes 5242880 | tf_op jit(solution)/shard_map/all_gather | solution.py:395
  148.6 34.5 %collective-permute-start.2 = (bf16[4,512,1024]{2,1,0:T(8,128)(2,1)}, bf16[4,512,1024]{2,1,0:T(8,128)(2,1)}, u32[]{:S(2)}, u32[]{:S(2)}) collective-permute-start(bf16[4,512,1024]{2,1,0:T(8,128)(2,1)} %bitcast.54), channel_id=1, source_target_pairs={{0,1},{1,0},{2,3},{3,2},{4,5},{5,4},{6,7},{7,6}} | collective-permute-start | bytes 12582920 | tf_op jit(solution)/shard_map/ppermute | solution.py:398
  182.5 204.7 %all-gather.40.cloned.1.call-start = ((), (), s32[]{:S(2)}) async-start(), calls=%async_computation.6 | async-start | bytes 5242880 | tf_op jit(solution)/shard_map/all_gather | solution.py:403
  182.6 38.7 %collective-permute-start.1 = (bf16[4,512,1024]{2,1,0:T(8,128)(2,1)}, bf16[4,512,1024]{2,1,0:T(8,128)(2,1)}, u32[]{:S(2)}, u32[]{:S(2)}) collective-permute-start(bf16[4,512,1024]{2,1,0:T(8,128)(2,1)} %bitcast.57), channel_id=1, source_target_pairs={{0,1},{1,0},{2,3},{3,2},{4,5},{5,4},{6,7},{7,6}} | collective-permute-start | bytes 12582920 | tf_op jit(solution)/shard_map/ppermute | solution.py:398
  216.9 325.3 %all-gather.42.cloned.1.call-start = ((), (), s32[]{:S(2)}) async-start(), calls=%async_computation.7 | async-start | bytes 10567680 | tf_op jit(solution)/shard_map/all_gather | solution.py:427
  417.9 250.2 %all-gather.44.cloned.1.call-start = ((), (), s32[]{:S(2)}) async-start(), calls=%async_computation.8 | async-start | bytes 10567680 | tf_op jit(solution)/shard_map/all_gather | solution.py:427
  418.4 88.6 %collective-permute-start.5 = (bf16[4,512,1024]{2,1,0:T(8,128)(2,1)}, bf16[4,512,1024]{2,1,0:T(8,128)(2,1)}, u32[]{:S(2)}, u32[]{:S(2)}) collective-permute-start(bf16[4,512,1024]{2,1,0:T(8,128)(2,1)} %bitcast.63), channel_id=1, source_target_pairs={{0,1},{1,0},{2,3},{3,2},{4,5},{5,4},{6,7},{7,6}} | collective-permute-start | bytes 12582920 | tf_op jit(solution)/shard_map/ppermute | solution.py:414
  542.2 251.8 %all-gather.46.cloned.1.call-start = ((), (), s32[]{:S(2)}) async-start(), calls=%async_computation.9 | async-start | bytes 10567680 | tf_op jit(solution)/shard_map/all_gather | solution.py:427
  542.4 103.4 %collective-permute-start.7 = (bf16[4,2064,512]{2,1,0:T(8,128)(2,1)}, bf16[4,2064,512]{2,1,0:T(8,128)(2,1)}, u32[]{:S(2)}, u32[]{:S(2)}) collective-permute-start(bf16[4,2064,512]{2,1,0:T(8,128)(2,1)} %bitcast.38), channel_id=1, source_target_pairs={{0,1},{1,0},{2,3},{3,2},{4,5},{5,4},{6,7},{7,6}} | collective-permute-start | bytes 25362440 | tf_op jit(solution)/shard_map/ppermute | solution.py:426
  542.5 85.6 %collective-permute-start.6 = (bf16[4,512,1024]{2,1,0:T(8,128)(2,1)}, bf16[4,512,1024]{2,1,0:T(8,128)(2,1)}, u32[]{:S(2)}, u32[]{:S(2)}) collective-permute-start(bf16[4,512,1024]{2,1,0:T(8,128)(2,1)} %bitcast.60), channel_id=1, source_target_pairs={{0,1},{1,0},{2,3},{3,2},{4,5},{5,4},{6,7},{7,6}} | collective-permute-start | bytes 12582920 | tf_op jit(solution)/shard_map/ppermute | solution.py:406
  668.1 251.8 %all-gather.48.cloned.1.call-start = ((), (), s32[]{:S(2)}) async-start(), calls=%async_computation.10 | async-start | bytes 10567680 | tf_op jit(solution)/shard_map/all_gather | solution.py:427
  668.4 106.5 %collective-permute-start.8 = (bf16[4,2064,512]{2,1,0:T(8,128)(2,1)}, bf16[4,2064,512]{2,1,0:T(8,128)(2,1)}, u32[]{:S(2)}, u32[]{:S(2)}) collective-permute-start(bf16[4,2064,512]{2,1,0:T(8,128)(2,1)} %bitcast.29), channel_id=1, source_target_pairs={{0,1},{1,0},{2,3},{3,2},{4,5},{5,4},{6,7},{7,6}} | collective-permute-start | bytes 25362440 | tf_op jit(solution)/shard_map/ppermute | solution.py:426
  794.0 251.7 %all-gather.50.cloned.1.call-start = ((), (), s32[]{:S(2)}) async-start(), calls=%async_computation.11 | async-start | bytes 10567680 | tf_op jit(solution)/shard_map/all_gather | solution.py:427
  794.3 106.4 %collective-permute-start.9 = (bf16[4,2064,512]{2,1,0:T(8,128)(2,1)}, bf16[4,2064,512]{2,1,0:T(8,128)(2,1)}, u32[]{:S(2)}, u32[]{:S(2)}) collective-permute-start(bf16[4,2064,512]{2,1,0:T(8,128)(2,1)} %bitcast.32), channel_id=1, source_target_pairs={{0,1},{1,0},{2,3},{3,2},{4,5},{5,4},{6,7},{7,6}} | collective-permute-start | bytes 25362440 | tf_op jit(solution)/shard_map/ppermute | solution.py:426
  919.9 174.4 %all-gather.52.cloned.1.call-start = ((), (), s32[]{:S(2)}) async-start(), calls=%async_computation.12 | async-start | bytes 5242880 | tf_op jit(solution)/shard_map/all_gather | solution.py:427
  920.3 106.7 %collective-permute-start.10 = (bf16[4,2064,512]{2,1,0:T(8,128)(2,1)}, bf16[4,2064,512]{2,1,0:T(8,128)(2,1)}, u32[]{:S(2)}, u32[]{:S(2)}) collective-permute-start(bf16[4,2064,512]{2,1,0:T(8,128)(2,1)} %bitcast.26), channel_id=1, source_target_pairs={{0,1},{1,0},{2,3},{3,2},{4,5},{5,4},{6,7},{7,6}} | collective-permute-start | bytes 25362440 | tf_op jit(solution)/shard_map/ppermute | solution.py:426
  1045.7 23.4 %collective-permute-start.11 = (bf16[4,2064,512]{2,1,0:T(8,128)(2,1)}, bf16[4,2064,512]{2,1,0:T(8,128)(2,1)}, u32[]{:S(2)}, u32[]{:S(2)}) collective-permute-start(bf16[4,2064,512]{2,1,0:T(8,128)(2,1)} %bitcast.35), channel_id=1, source_target_pairs={{0,1},{1,0},{2,3},{3,2},{4,5},{5,4},{6,7},{7,6}} | collective-permute-start | bytes 25362440 | tf_op jit(solution)/shard_map/ppermute | solution.py:426
  1045.9 97.4 %all-gather.54.cloned.1.call-start = ((), (), s32[]{:S(2)}) async-start(), calls=%async_computation.13 | async-start | bytes 5324800 | tf_op jit(solution)/shard_map/all_gather | solution.py:431
  (4 other events, 34.5 us)
Sparse Core Ops, SparseCore 0:
  10.3 49.5 all-gather.27
  61.7 46.7 all-gather.31
  110.3 46.6 all-gather.33
  158.6 46.7 all-gather.29
  207.0 76.8 all-gather.35
  285.5 53.1 all-gather.37
  340.5 46.6 all-gather.39
  418.0 124.0 all-gather.41
  543.9 124.1 all-gather.43
  669.7 124.1 all-gather.45
  795.7 124.1 all-gather.47
  921.5 124.1 all-gather.49
  1047.5 46.7 all-gather.51
  1095.9 47.3 all-gather.53
